TPU v7x, 32 devices: a whole 2x2x4 slice. The times are simulated.
32 devices in a mesh: section: 4 (over y, x), dp: 8 (over z, core).
Axes of the slice: x: 2, y: 2, z: 4, core: 2. Of those that a mesh axis runs over, the one named last changes fastest.
Arguments:
- saved_inputs: bfloat16 [4, 2, 1024, 320], P('section', None, 'dp'), may hold values from -6 to 6
- timesteps: int32 [2, 1024], P(None, 'dp'), may hold values from 0 to 999
- time_table: bfloat16 [1000, 320], replicated, may hold values from -6 to 6
- skip_weight: bfloat16 [4, 320, 320], P('section'), may hold values from -0.3125 to 0.3125
- ff_in: bfloat16 [4, 1280, 320], P('section'), may hold values from -0.3125 to 0.3125
- ff_out: bfloat16 [4, 1280, 320], P('section'), may hold values from -0.15625 to 0.15625
- output_cotangent: bfloat16 [2, 1024, 320], P(None, 'dp'), may hold values from -6 to 6
Outputs:
- input_grads: bfloat16 [4, 2, 1024, 320], P('section', None, 'dp')
- skip_weight_grad: float32 [4, 102400], P('section', 'dp')
- ff_in_grad: float32 [4, 1280, 320], P('section', 'dp')
- ff_out_grad: float32 [4, 1280, 320], P('section', 'dp')
All inputs are finite; a program needn't handle non-finite values.
Results may differ from a plain program's by a relative error of at most 0.01.
Values may be sent and summed in bfloat16 or wider, within the bound.
A program may use at most 128 MiB of HBM per device.

v0:
```python
import jax
import jax.numpy as jnp
from jax import lax
from jax.sharding import PartitionSpec as P

EPS = 1e-06


def from_partner(shard, axis, stride):
    return lax.ppermute(shard, axis, [(i, i ^ 1 << stride) for i in range(lax.axis_size(axis))])


def passed_along(value, axis, steps):
    count = lax.axis_size(axis)
    first, last = (max(0, -steps), min(count, count - steps))
    return lax.ppermute(value, axis, [(source, source + steps) for source in range(first, last)])


def contract(left, right, dims):
    return lax.dot_general(
        left, right, ((dims[0], dims[1]), ((), ())), preferred_element_type=jnp.float32
    )


def forward(inputs, source, w_skip, w_in, w_out):
    united = inputs.astype(jnp.float32) + jnp.dot(
        source, w_skip, preferred_element_type=jnp.float32
    )
    recip = lax.rsqrt(jnp.mean(united * united, axis=-1, keepdims=True) + EPS)
    normed = (united * recip).astype(jnp.bfloat16)
    preact = contract(normed, w_in, ((1,), (1,)))
    active = jax.nn.silu(preact).astype(jnp.bfloat16)
    output = united + jnp.dot(active, w_out, preferred_element_type=jnp.float32)
    return (united, recip, normed, preact, active, output)


def put_micro(buffer, value, index, valid):
    updated = lax.dynamic_update_index_in_dim(buffer, value, index, 0)
    return jnp.where(valid, updated, buffer)


def shards(saved_inputs, timesteps, time_table, skip_weight, ff_in, ff_out, output_cotangent):
    section = lax.axis_index("section")
    n_micro = saved_inputs.shape[1]
    rows = saved_inputs.shape[2]
    width = saved_inputs.shape[3]
    hidden = ff_in.shape[1]
    inputs = saved_inputs[0]
    w_skip = skip_weight[0]
    w_in = ff_in[0]
    w_out = ff_out[0]
    bit_order = (0, 1)
    levels = lax.broadcasted_iota(jnp.int32, (1, time_table.shape[0]), 1)
    embed_list = []
    value_list = []
    for micro in range(n_micro):
        onehot = (timesteps[micro][:, None] == levels).astype(jnp.bfloat16)
        embed = jnp.dot(onehot, time_table, preferred_element_type=jnp.float32).astype(jnp.bfloat16)
        embed_list.append(embed)
        value_list.append(
            forward(inputs[micro], embed, w_skip, w_in, w_out)[5].astype(jnp.bfloat16)
        )
    embeds = jnp.stack(embed_list)
    values = jnp.stack(value_list)
    received = values
    for bit in bit_order:
        received = from_partner(received, "section", bit)
    sources = jnp.where(section >= 2, received, embeds)

    def active_path(operands):
        grad_out, own_input, source = operands
        united, recip, normed, preact, active, output = forward(
            own_input, source, w_skip, w_in, w_out
        )
        grad_low = grad_out.astype(jnp.bfloat16)
        grad_act = contract(grad_low, w_out, ((1,), (1,)))
        sigma = jax.nn.sigmoid(preact)
        grad_pre = (grad_act * sigma * (1.0 + preact * (1.0 - sigma))).astype(jnp.bfloat16)
        grad_norm = jnp.dot(grad_pre, w_in, preferred_element_type=jnp.float32)
        grad_united = (
            grad_out
            + recip * grad_norm
            - united * recip**3 * jnp.mean(grad_norm * united, axis=-1, keepdims=True)
        )
        united_low = grad_united.astype(jnp.bfloat16)
        d_skip = contract(source, united_low, ((0,), (0,)))
        grad_source = contract(united_low, w_skip, ((1,), (1,))).astype(jnp.bfloat16)
        extra = (contract(grad_pre, normed, ((0,), (0,))), contract(active, grad_low, ((0,), (0,))))
        return (united_low, grad_source, d_skip) + extra

    def resting_path(operands):
        low_rows = jnp.zeros((rows, width), jnp.bfloat16)
        base = (low_rows, low_rows, jnp.zeros((width, width), jnp.float32))
        extra = (jnp.zeros((hidden, width), jnp.float32), jnp.zeros((hidden, width), jnp.float32))
        return base + extra

    chain = jnp.zeros((rows, width), jnp.bfloat16)
    skip_store = jnp.zeros((n_micro, rows, width), jnp.bfloat16)
    grad_store = jnp.zeros((n_micro, rows, width), jnp.bfloat16)
    total_skip = jnp.zeros((width, width), jnp.float32)
    total_in = jnp.zeros((hidden, width), jnp.float32)
    total_out = jnp.zeros((hidden, width), jnp.float32)
    for tick in range(n_micro + 3):
        micro = tick - (3 - section)
        valid = (micro >= 0) & (micro < n_micro)
        index = jnp.clip(micro, 0, n_micro - 1)
        own_input = lax.dynamic_index_in_dim(inputs, index, 0, keepdims=False)
        source = lax.dynamic_index_in_dim(sources, index, 0, keepdims=False)
        carried = lax.dynamic_index_in_dim(skip_store, index, 0, keepdims=False).astype(jnp.float32)
        upstream = chain.astype(jnp.float32) + jnp.where(section < 2, carried, 0.0)
        top = lax.dynamic_index_in_dim(output_cotangent, index, 0, keepdims=False).astype(
            jnp.float32
        )
        grad_out = jnp.where(section == 3, top, upstream)
        parts = lax.cond(valid, active_path, resting_path, (grad_out, own_input, source))
        united_low = parts[0]
        grad_store = put_micro(grad_store, united_low, index, valid)
        total_skip = total_skip + parts[2]
        total_in = total_in + parts[3]
        total_out = total_out + parts[4]
        chain = passed_along(united_low, "section", -1)
        back = parts[1]
        for bit in bit_order:
            back = from_partner(back, "section", bit)
        sender = tick - section
        receive = (section < 2) & (sender >= 0) & (sender < n_micro)
        skip_store = put_micro(skip_store, back, jnp.clip(sender, 0, n_micro - 1), receive)
    grad_in, grad_out_w, grad_skip = (
        lax.psum_scatter(total_in, "dp", scatter_dimension=0, tiled=True),
        lax.psum_scatter(total_out, "dp", scatter_dimension=0, tiled=True),
        lax.psum_scatter(total_skip.reshape(-1), "dp", scatter_dimension=0, tiled=True),
    )
    return (grad_store[None], grad_skip[None], grad_in[None], grad_out_w[None])


def solution(mesh):
    in_specs = (
        P("section", None, "dp", None),
        P(None, "dp"),
        P(),
        P("section", None, None),
        P("section", None, None),
        P("section", None, None),
        P(None, "dp", None),
    )
    out_specs = (
        P("section", None, "dp", None),
        P("section", "dp"),
        P("section", "dp", None),
        P("section", "dp", None),
    )
    return jax.shard_map(shards, mesh=mesh, in_specs=in_specs, out_specs=out_specs, check_vma=False)
```

profile of v0, /device:TPU:0, one launch (start us, length us, event | category | flops | bytes accessed | tf_op | source)
XLA Modules:
  0.0 272.1 jit_solution(12050596302691011541)
XLA Ops:
  8.7 1.3 multiply_reduce_fusion.10
  12.4 3.0 %collective-permute-start = (bf16[2,128,320]{1,2,0:T(8,128)(2,1)S(1)}, bf16[2,128,320]{1,2,0:T(8,128)(2,1)S(1)}, u32[]{:S(2)}, u32[]{:S(2)}) collective-permute-start(bf16[2,128,320]{1,2,0:T(8,128)(2,1)S(1)} %pad_maximum_fusion), channel_id=1, source_target_pairs={{0,8},{8,0},{16,24},{24,16},{1,9},{9,1},{17,25},{25,17},{2,10},{10... | collective-permute-start | bytes 491528 | tf_op jit(solution)/shard_map/ppermute | solution.py:10
  15.4 4.2 %collective-permute-done = bf16[2,128,320]{1,2,0:T(8,128)(2,1)S(1)} collective-permute-done((bf16[2,128,320]{1,2,0:T(8,128)(2,1)S(1)}, bf16[2,128,320]{1,2,0:T(8,128)(2,1)S(1)}, u32[]{:S(2)}, u32[]{:S(2)}) %collective-permute-start) | collective-permute-done | bytes 163872 | tf_op jit(solution)/shard_map/ppermute | solution.py:10
  19.6 1.8 collective-permute-start.1
  21.4 1.3 copy.55
  23.3 1.7 collective-permute-done.1
  26.3 3.5 %conditional.5 = (bf16[128,320]{0,1:T(8,128)(2,1)}, bf16[128,320]{0,1:T(8,128)(2,1)S(1)}, f32[320,320]{1,0:T(8,128)}, f32[1280,320]{0,1:T(8,128)S(1)}, f32[1280,...) conditional(s32[]{:T(128)} %convert_element_type.325, () %tuple.76, (bf16[2,128,320]{1,2,0:T(8,128)(2,1)}, s32[]{:T(128)}, ...), branch_computations={%region_2.3_spmd, %region_3.6_spmd} | conditional | flops 606249344 | bytes 17243340 | solution.py:115
  29.8 1.7 collective-permute-start.2
  31.5 1.3 collective-permute-start.4
  32.8 2.1 collective-permute-done.2
  34.9 8.5 %collective-permute-start.3 = (bf16[128,320]{0,1:T(8,128)(2,1)}, bf16[128,320]{0,1:T(8,128)(2,1)}, u32[]{:S(2)}, u32[]{:S(2)}) collective-permute-start(bf16[128,320]{0,1:T(8,128)(2,1)} %collective-permute-done.2), channel_id=1, source_target_pairs={{0,16},{8,24},{16,0},{24,8},{1,17},{9,25},{17,1},{25,9},{2,18},{10... | collective-permute-start | bytes 245768 | tf_op jit(solution)/shard_map/ppermute | solution.py:10
  43.4 1.6 convert_element_type.339
  46.8 1.5 bitcast_dynamic-update-slice_fusion.1
  49.7 4.8 %conditional.6 = (bf16[128,320]{0,1:T(8,128)(2,1)}, bf16[128,320]{0,1:T(8,128)(2,1)S(1)}, f32[320,320]{1,0:T(8,128)}, f32[1280,320]{0,1:T(8,128)}, f32[1280,320]{0,1:T(8,128)}, /*index=5*/bf16[1,128,320]{1,2,0:T(8,128)(2,1)}) conditional(s32[]{:T(128)} %convert_element_type.338, () %tuple.78, (bf16[2,128,320]{1,2,0:T(8,128)(2,1)}, s32[]{:T(128)}, ...), branch_computations={%region_6.7_spmd, %region_7.10_spmd} | conditional | flops 606208384 | bytes 16301140 | solution.py:115
  51.2 1.3 broadcast.301
  52.5 1.3 broadcast.301.clone
  54.5 1.3 collective-permute-start.5
  55.8 1.3 collective-permute-start.7
  57.1 1.8 collective-permute-done.5
  58.9 10.6 %collective-permute-start.6 = (bf16[128,320]{0,1:T(8,128)(2,1)S(1)}, bf16[128,320]{0,1:T(8,128)(2,1)S(1)}, u32[]{:S(2)}, u32[]{:S(2)}) collective-permute-start(bf16[128,320]{0,1:T(8,128)(2,1)S(1)} %collective-permute-done.5), channel_id=1, source_target_pairs={{0,16},{8,24},{16,0},{24,8},{1,17},{9,25},{17,1},{25,9},{2,18},{10... | collective-permute-start | bytes 245768 | tf_op jit(solution)/shard_map/ppermute | solution.py:10
  70.2 1.7 collective-permute-done.6
  71.9 1.5 fusion.120
  73.5 3.6 %conditional.7 = (bf16[128,320]{0,1:T(8,128)(2,1)}, bf16[128,320]{0,1:T(8,128)(2,1)S(1)}, f32[320,320]{1,0:T(8,128)}, f32[1280,320]{0,1:T(8,128)S(1)}, f32[1280,...) conditional(s32[]{:T(128)} %convert_element_type.340, () %tuple.80, (bf16[2,128,320]{1,2,0:T(8,128)(2,1)}, s32[]{:T(128)}, ...), branch_computations={%region_10.11_spmd, %region_11.14_spmd} | conditional | flops 606208384 | bytes 16301140 | solution.py:115
  75.1 1.4 broadcast.307.clone
  77.1 9.8 %collective-permute-start.8 = (bf16[128,320]{0,1:T(8,128)(2,1)S(1)}, bf16[128,320]{0,1:T(8,128)(2,1)}, u32[]{:S(2)}, u32[]{:S(2)}) collective-permute-start(bf16[128,320]{0,1:T(8,128)(2,1)S(1)} %get-tuple-element.599), channel_id=1, source_target_pairs={{0,8},{8,0},{16,24},{24,16},{1,9},{9,1},{17,25},{25,17},{2,10},{10... | collective-permute-start | bytes 245768 | tf_op jit(solution)/shard_map/ppermute | solution.py:10
  86.9 1.3 collective-permute-start.10
  89.4 2.9 %collective-permute-start.9 = (bf16[128,320]{0,1:T(8,128)(2,1)}, bf16[128,320]{0,1:T(8,128)(2,1)}, u32[]{:S(2)}, u32[]{:S(2)}) collective-permute-start(bf16[128,320]{0,1:T(8,128)(2,1)} %collective-permute-done.8), channel_id=1, source_target_pairs={{0,16},{8,24},{16,0},{24,8},{1,17},{9,25},{17,1},{25,9},{2,18},{10... | collective-permute-start | bytes 245768 | tf_op jit(solution)/shard_map/ppermute | solution.py:10
  93.6 1.6 convert_element_type.343
  95.1 1.6 fusion.119
  96.7 13.5 %conditional.8 = (bf16[128,320]{0,1:T(8,128)(2,1)}, bf16[128,320]{0,1:T(8,128)(2,1)S(1)}, f32[320,320]{1,0:T(8,128)}, f32[1280,320]{0,1:T(8,128)}, f32[1280,320]{0,1:T(8,128)}, /*index=5*/bf16[1,128,320]{1,2,0:T(8,128)(2,1)}) conditional(s32[]{:T(128)} %convert_element_type.342, () %tuple.82, (bf16[2,128,320]{1,2,0:T(8,128)(2,1)}, s32[]{:T(128)}, ...), branch_computations={%region_14.15_spmd, %region_15.18_spmd} | conditional | flops 606208384 | bytes 16301140 | solution.py:115
  103.5 1.9 fusion.66
  105.4 1.6 fusion.73
  107.0 1.6 fusion.62
  108.7 1.5 copy.121
  111.3 1.3 collective-permute-start.13
  112.6 2.1 collective-permute-done.11
  115.7 2.2 collective-permute-done.13
  119.1 11.4 %conditional.9 = (f32[320,320]{1,0:T(8,128)S(1)}, f32[1280,320]{0,1:T(8,128)S(1)}, f32[1280,320]{0,1:T(8,128)}, bf16[1,128,320]{1,2,0:T(8,128)(2,1)}) conditional(s32[]{:T(128)} %convert_element_type.344, () %tuple.84, (bf16[2,128,320]{1,2,0:T(8,128)(2,1)}, s32[]{:T(128)}, bf16[2,128,320]{1,2,0:T(8,128)(2,1)}, s32[]{:T(128)}, pred[]{:T(512)}, ...), branch_computations={%region_18.19_spmd, %region_19.22_spmd.clone} | conditional | flops 579993984 | bytes 16997552 | solution.py:115
  121.5 1.6 fusion.89
  128.8 1.6 fusion.80
  131.2 1.7 add_add_fusion.2
  134.1 3.9 %add_add_fusion.1 = f32[1280,320]{0,1:T(8,128)S(1)} fusion(f32[1280,320]{0,1:T(8,128)} %copy-done.4, f32[1280,320]{0,1:T(8,128)} %get-tuple-element.613, f32[1280,320]{0,1:T(8,128)} %copy-done.3, f32[1280,320]{0,1:T(8,128)} %copy-done.2, f32[1280,320]{0,1:T(8,128)} %get-tuple-element.611), kind=kLoop, calls=%fused_computation.160 | loop fusion | flops 1638400 | bytes 9830400 | tf_op jit(solution)/shard_map/add | solution.py:119
  137.9 1.8 copy.63
  139.8 3.9 %add_add_fusion = f32[1280,320]{0,1:T(8,128)S(1)} fusion(f32[1280,320]{0,1:T(8,128)} %get-tuple-element.619, f32[1280,320]{0,1:T(8,128)} %get-tuple-element.618, f32[1280,320]{0,1:T(8,128)} %get-tuple-element.617, f32[1280,320]{0,1:T(8,128)} %get-tuple-element.615, f32[1280,320]{0,1:T(8,128)} %get-tuple-element.616), kind=kLoop, calls=%fused_computation.159 | loop fusion | flops 1638400 | bytes 9830400 | tf_op jit(solution)/shard_map/add | solution.py:120
  143.7 1.8 copy.65
  149.4 37.9 %all-reduce.3.cloned.1.call-done = f32[102400]{0:T(1024)} async-done(((f32[102400]{0:T(1024)}), f32[102400]{0:T(1024)}) %all-reduce.3.cloned.1.call-update) | async-done | bytes 409616
  188.9 38.1 %reduce-scatter.7.cloned.1.call-done = f32[160,320]{1,0:T(8,128)} async-done(((f32[1280,320]{1,0:T(8,128)}), f32[160,320]{1,0:T(8,128)}) %reduce-scatter.7.cloned.1.call-update) | async-done | bytes 204816
  228.9 34.7 %reduce-scatter.9.cloned.1.call-done = f32[160,320]{1,0:T(8,128)} async-done(((f32[1280,320]{1,0:T(8,128)}), f32[160,320]{1,0:T(8,128)}) %reduce-scatter.9.cloned.1.call-update) | async-done | bytes 204816
  (113 shorter events, 48.6 us)
Async XLA Ops:
  7.2 1.1 copy-start
  7.2 3.3 %copy-start.6 = (bf16[1,2,128,320]{2,3,1,0:T(8,128)(2,1)S(1)}, bf16[1,2,128,320]{2,3,1,0:T(8,128)(2,1)}, u32[]{:S(2)}) copy-start(bf16[1,2,128,320]{2,3,1,0:T(8,128)(2,1)} %param.17) | copy-start | bytes 491524
  7.2 3.3 %copy-start.1 = (bf16[1,320,320]{2,1,0:T(8,128)(2,1)S(1)}, bf16[1,320,320]{2,1,0:T(8,128)(2,1)}, u32[]{:S(2)}) copy-start(bf16[1,320,320]{2,1,0:T(8,128)(2,1)} %param.20) | copy-start | bytes 614404
  7.2 3.6 %copy-start.17 = (bf16[1,1280,320]{1,2,0:T(8,128)(2,1)S(1)}, bf16[1,1280,320]{1,2,0:T(8,128)(2,1)}, u32[]{:S(2)}) copy-start(bf16[1,1280,320]{1,2,0:T(8,128)(2,1)} %param.22) | copy-start | bytes 2457604
  7.2 3.6 %copy-start.18 = (bf16[1,1280,320]{1,2,0:T(8,128)(2,1)S(1)}, bf16[1,1280,320]{1,2,0:T(8,128)(2,1)}, u32[]{:S(2)}) copy-start(bf16[1,1280,320]{1,2,0:T(8,128)(2,1)} %param.21) | copy-start | bytes 2457604
  7.2 180.1 %all-reduce.3.cloned.1.call-start = ((), (), s32[]{:S(2)}) async-start(), calls=%async_computation.4 | async-start | bytes 819200
  12.4 7.2 %collective-permute-start = (bf16[2,128,320]{1,2,0:T(8,128)(2,1)S(1)}, bf16[2,128,320]{1,2,0:T(8,128)(2,1)S(1)}, u32[]{:S(2)}, u32[]{:S(2)}) collective-permute-start(bf16[2,128,320]{1,2,0:T(8,128)(2,1)S(1)} %pad_maximum_fusion), channel_id=1, source_target_pairs={{0,8},{8,0},{16,24},{24,16},{1,9},{9,1},{17,25},{25,17},{2,10},{10... | collective-permute-start | bytes 491528 | tf_op jit(solution)/shard_map/ppermute | solution.py:10
  19.6 5.4 %collective-permute-start.1 = (bf16[2,128,320]{1,2,0:T(8,128)(2,1)S(1)}, bf16[2,128,320]{1,2,0:T(8,128)(2,1)S(1)}, u32[]{:S(2)}, u32[]{:S(2)}) collective-permute-start(bf16[2,128,320]{1,2,0:T(8,128)(2,1)S(1)} %collective-permute-done), channel_id=1, source_target_pairs={{0,16},{8,24},{16,0},{24,8},{1,17},{9,25},{17,1},{25,9},{2,18},{10... | collective-permute-start | bytes 491528 | tf_op jit(solution)/shard_map/ppermute | solution.py:10
  29.8 19.8 %copy-start.2 = (f32[1280,320]{0,1:T(8,128)}, f32[1280,320]{0,1:T(8,128)S(1)}, u32[]{:S(2)}) copy-start(f32[1280,320]{0,1:T(8,128)S(1)} %get-tuple-element.610) | copy-start | bytes 4915204
  29.8 5.1 %collective-permute-start.2 = (bf16[128,320]{0,1:T(8,128)(2,1)S(1)}, bf16[128,320]{0,1:T(8,128)(2,1)}, u32[]{:S(2)}, u32[]{:S(2)}) collective-permute-start(bf16[128,320]{0,1:T(8,128)(2,1)S(1)} %get-tuple-element.593), channel_id=1, source_target_pairs={{0,8},{8,0},{16,24},{24,16},{1,9},{9,1},{17,25},{25,17},{2,10},{10... | collective-permute-start | bytes 245768 | tf_op jit(solution)/shard_map/ppermute | solution.py:10
  31.5 11.9 %collective-permute-start.4 = (bf16[128,320]{0,1:T(8,128)(2,1)}, bf16[128,320]{0,1:T(8,128)(2,1)}, u32[]{:S(2)}, u32[]{:S(2)}) collective-permute-start(bf16[128,320]{0,1:T(8,128)(2,1)} %get-tuple-element.594), channel_id=1, source_target_pairs={{8,0},{16,8},{24,16},{9,1},{17,9},{25,17},{10,2},{18,10},{26,18},{... | collective-permute-start | bytes 245768 | tf_op jit(solution)/shard_map/ppermute | solution.py:16
  34.9 11.3 %collective-permute-start.3 = (bf16[128,320]{0,1:T(8,128)(2,1)}, bf16[128,320]{0,1:T(8,128)(2,1)}, u32[]{:S(2)}, u32[]{:S(2)}) collective-permute-start(bf16[128,320]{0,1:T(8,128)(2,1)} %collective-permute-done.2), channel_id=1, source_target_pairs={{0,16},{8,24},{16,0},{24,8},{1,17},{9,25},{17,1},{25,9},{2,18},{10... | collective-permute-start | bytes 245768 | tf_op jit(solution)/shard_map/ppermute | solution.py:10
  54.5 4.4 %collective-permute-start.5 = (bf16[128,320]{0,1:T(8,128)(2,1)S(1)}, bf16[128,320]{0,1:T(8,128)(2,1)S(1)}, u32[]{:S(2)}, u32[]{:S(2)}) collective-permute-start(bf16[128,320]{0,1:T(8,128)(2,1)S(1)} %get-tuple-element.596), channel_id=1, source_target_pairs={{0,8},{8,0},{16,24},{24,16},{1,9},{9,1},{17,25},{25,17},{2,10},{10... | collective-permute-start | bytes 245768 | tf_op jit(solution)/shard_map/ppermute | solution.py:10
  55.8 13.7 %collective-permute-start.7 = (bf16[128,320]{0,1:T(8,128)(2,1)}, bf16[128,320]{0,1:T(8,128)(2,1)S(1)}, u32[]{:S(2)}, u32[]{:S(2)}) collective-permute-start(bf16[128,320]{0,1:T(8,128)(2,1)} %get-tuple-element.597), channel_id=1, source_target_pairs={{8,0},{16,8},{24,16},{9,1},{17,9},{25,17},{10,2},{18,10},{26,18},{... | collective-permute-start | bytes 245768 | tf_op jit(solution)/shard_map/ppermute | solution.py:16
  58.9 13.0 %collective-permute-start.6 = (bf16[128,320]{0,1:T(8,128)(2,1)S(1)}, bf16[128,320]{0,1:T(8,128)(2,1)S(1)}, u32[]{:S(2)}, u32[]{:S(2)}) collective-permute-start(bf16[128,320]{0,1:T(8,128)(2,1)S(1)} %collective-permute-done.5), channel_id=1, source_target_pairs={{0,16},{8,24},{16,0},{24,8},{1,17},{9,25},{17,1},{25,9},{2,18},{10... | collective-permute-start | bytes 245768 | tf_op jit(solution)/shard_map/ppermute | solution.py:10
  77.1 19.6 %copy-start.3 = (f32[1280,320]{0,1:T(8,128)}, f32[1280,320]{0,1:T(8,128)S(1)}, u32[]{:S(2)}) copy-start(f32[1280,320]{0,1:T(8,128)S(1)} %get-tuple-element.612) | copy-start | bytes 4915204
  77.1 12.3 %collective-permute-start.8 = (bf16[128,320]{0,1:T(8,128)(2,1)S(1)}, bf16[128,320]{0,1:T(8,128)(2,1)}, u32[]{:S(2)}, u32[]{:S(2)}) collective-permute-start(bf16[128,320]{0,1:T(8,128)(2,1)S(1)} %get-tuple-element.599), channel_id=1, source_target_pairs={{0,8},{8,0},{16,24},{24,16},{1,9},{9,1},{17,25},{25,17},{2,10},{10... | collective-permute-start | bytes 245768 | tf_op jit(solution)/shard_map/ppermute | solution.py:10
  86.9 6.6 %collective-permute-start.10 = (bf16[128,320]{0,1:T(8,128)(2,1)}, bf16[128,320]{0,1:T(8,128)(2,1)}, u32[]{:S(2)}, u32[]{:S(2)}) collective-permute-start(bf16[128,320]{0,1:T(8,128)(2,1)} %get-tuple-element.600), channel_id=1, source_target_pairs={{8,0},{16,8},{24,16},{9,1},{17,9},{25,17},{10,2},{18,10},{26,18},{... | collective-permute-start | bytes 245768 | tf_op jit(solution)/shard_map/ppermute | solution.py:16
  89.4 5.7 %collective-permute-start.9 = (bf16[128,320]{0,1:T(8,128)(2,1)}, bf16[128,320]{0,1:T(8,128)(2,1)}, u32[]{:S(2)}, u32[]{:S(2)}) collective-permute-start(bf16[128,320]{0,1:T(8,128)(2,1)} %collective-permute-done.8), channel_id=1, source_target_pairs={{0,16},{8,24},{16,0},{24,8},{1,17},{9,25},{17,1},{25,9},{2,18},{10... | collective-permute-start | bytes 245768 | tf_op jit(solution)/shard_map/ppermute | solution.py:10
  97.8 2.9 %copy-start.15 = (bf16[1280,320]{1,0:T(8,128)(2,1)S(1)}, bf16[1280,320]{1,0:T(8,128)(2,1)}, u32[]{:S(2)}) copy-start(bf16[1280,320]{1,0:T(8,128)(2,1)} %get-tuple-element.542) | copy-start | bytes 2457604 | tf_op jit(solution)/shard_map/cond
  110.2 4.4 %collective-permute-start.11 = (bf16[128,320]{0,1:T(8,128)(2,1)S(1)}, bf16[128,320]{0,1:T(8,128)(2,1)S(1)}, u32[]{:S(2)}, u32[]{:S(2)}) collective-permute-start(bf16[128,320]{0,1:T(8,128)(2,1)S(1)} %get-tuple-element.602), channel_id=1, source_target_pairs={{0,8},{8,0},{16,24},{24,16},{1,9},{9,1},{17,25},{25,17},{2,10},{10... | collective-permute-start | bytes 245768 | tf_op jit(solution)/shard_map/ppermute | solution.py:10
  111.3 6.5 %collective-permute-start.13 = (bf16[128,320]{0,1:T(8,128)(2,1)}, bf16[128,320]{0,1:T(8,128)(2,1)S(1)}, u32[]{:S(2)}, u32[]{:S(2)}) collective-permute-start(bf16[128,320]{0,1:T(8,128)(2,1)} %get-tuple-element.603), channel_id=1, source_target_pairs={{8,0},{16,8},{24,16},{9,1},{17,9},{25,17},{10,2},{18,10},{26,18},{... | collective-permute-start | bytes 245768 | tf_op jit(solution)/shard_map/ppermute | solution.py:16
  114.6 4.4 %collective-permute-start.12 = (bf16[128,320]{0,1:T(8,128)(2,1)S(1)}, bf16[128,320]{0,1:T(8,128)(2,1)S(1)}, u32[]{:S(2)}, u32[]{:S(2)}) collective-permute-start(bf16[128,320]{0,1:T(8,128)(2,1)S(1)} %collective-permute-done.11), channel_id=1, source_target_pairs={{0,16},{8,24},{16,0},{24,8},{1,17},{9,25},{17,1},{25,9},{2,18},{10... | collective-permute-start | bytes 245768 | tf_op jit(solution)/shard_map/ppermute | solution.py:10
  119.1 1.1 copy-start.20
  120.2 4.6 %copy-start.16 = (bf16[1280,320]{1,0:T(8,128)(2,1)S(1)}, bf16[1280,320]{1,0:T(8,128)(2,1)}, u32[]{:S(2)}) copy-start(bf16[1280,320]{1,0:T(8,128)(2,1)} %get-tuple-element.637) | copy-start | bytes 2457604 | tf_op jit(solution)/shard_map/cond
  121.5 4.3 %copy-start.5 = (f32[128,320]{0,1:T(8,128)}, f32[128,320]{0,1:T(8,128)S(1)}, u32[]{:S(2)}) copy-start(f32[128,320]{0,1:T(8,128)S(1)} %get-tuple-element.938) | copy-start | bytes 491524 | tf_op jit(solution)/shard_map/cond
  130.5 0.8 copy-start.7
  130.5 3.5 %copy-start.4 = (f32[1280,320]{0,1:T(8,128)}, f32[1280,320]{0,1:T(8,128)S(1)}, u32[]{:S(2)}) copy-start(f32[1280,320]{0,1:T(8,128)S(1)} %get-tuple-element.614) | copy-start | bytes 4915204
  134.0 92.9 %reduce-scatter.7.cloned.1.call-start = ((), (), s32[]{:S(2)}) async-start(), calls=%async_computation.2 | async-start | bytes 2211840
  139.7 123.8 %reduce-scatter.9.cloned.1.call-start = ((), (), s32[]{:S(2)}) async-start(), calls=%async_computation.3 | async-start | bytes 2211840
  145.5 0.7 copy-start.21
  149.4 116.1 %copy-start.19 = (bf16[1,2,128,320]{2,3,1,0:T(8,128)(2,1)}, bf16[1,2,128,320]{2,3,1,0:T(8,128)(2,1)S(1)}, u32[]{:S(2)}) copy-start(bf16[1,2,128,320]{2,3,1,0:T(8,128)(2,1)S(1)} %bitcast_dynamic-update-slice_fusion) | copy-start | bytes 491524
Sparse Core Ops, SparseCore 0:
  134.1 53.1 all-reduce.2
  189.6 37.2 reduce-scatter.6
  229.3 34.2 reduce-scatter.8
where the time goes:
time: 273 us; the launch traced here: 272 us
  waiting for transfers between devices  131 us (48%)
  starting transfers between devices  47.1 us (17%)
  local copies, waits for them, and re-layouts  33.2 us (12%)
  other arithmetic  26.8 us (10%)
  matrix products  19.7 us (7%)
  between operations  14.6 us (5%)
    unnamed x6, waiting for transfers between devices  111 us
    ppermute x10, starting transfers between devices, from_partner(): lax.ppermute(shard, axis, [(i, i ^ 1 << stride) for i in range(lax.axis_s...  41.8 us
    ppermute x10, waiting for transfers between devices, from_partner(): lax.ppermute(shard, axis, [(i, i ^ 1 << stride) for i in range(lax.axis_s...  16.5 us
    another operation x19, local copies, waits for them, and re-layouts  12.8 us
    unnamed x33, local copies, waits for them, and re-layouts  12.4 us
    dot_general x11, matrix products, contract(): lax.dot_general(left, right, ((dims[0], dims[1]), ((), ())), preferred_el...  12.1 us
    select_n x9, other arithmetic, put_micro(): return jnp.where(valid, updated, buffer)  8.34 us
  transfers between devices with their start and end apart: 17, of which 14 were waited for; matrix products, arithmetic and copies ran while one was open for 9% of the time, Pallas kernels for 0%

commit v1 on v0

v1 whole, which is shorter than its diff:
```python
import functools

import jax
import jax.numpy as jnp
from jax import lax
from jax.experimental import pallas as pl
from jax.experimental.pallas import tpu as pltpu
from jax.sharding import PartitionSpec as P

EPS = 1e-06
MESH = pl.DeviceIdType.MESH
F32 = jnp.float32
BF16 = jnp.bfloat16


def contract(left, right, dims):
    return lax.dot_general(
        left, right, ((dims[0], dims[1]), ((), ())), preferred_element_type=jnp.float32
    )


def kernel(n_section, n_dp, scatter, *refs):
    (x, ts, table, w_skip, w_in, w_out, cot) = refs[:7]
    (ig, g_skip, g_in, g_out) = refs[7:11]
    (zbuf, ybuf, ubuf, rbuf, nbuf, abuf, dbuf, gbuf, lowbuf, gpbuf, cbuf, kbuf, skbuf) = refs[11:24]
    (vs, vr, cs, cr, ks, kr) = refs[24:30]
    rs = refs[30:]
    sec = lax.axis_index("section")
    dp = lax.axis_index("dp")
    n_micro, rows, width = cot.shape
    hidden = w_in.shape[1]
    half = n_section // 2
    pairs = n_dp // 2
    core = lax.rem(dp, 2)
    place = lax.div(dp, 2)
    mate = dp + 1 - 2 * core

    def remote(src, dst, send, recv, **where):
        return pltpu.make_async_remote_copy(
            src_ref=src, dst_ref=dst, send_sem=send, recv_sem=recv, device_id=where, device_id_type=MESH
        )

    barrier = pltpu.get_barrier_semaphore()
    count = 0
    for k in range(1, n_section):
        pl.semaphore_signal(
            barrier, inc=1, device_id={"section": lax.rem(sec + k, n_section)}, device_id_type=MESH
        )
        count += 1
    if scatter:
        pl.semaphore_signal(barrier, inc=1, device_id={"dp": mate}, device_id_type=MESH)
        count += 1
        for k in range(1, pairs):
            other = lax.rem(place + k, pairs) * 2 + core
            pl.semaphore_signal(barrier, inc=1, device_id={"dp": other}, device_id_type=MESH)
            count += 1

    mirror = n_section - 1 - sec
    below = lax.max(sec - 1, 0)
    values = [remote(ybuf.at[m], zbuf.at[m], vs.at[m], vr.at[m], section=mirror) for m in range(n_micro)]
    chains = [remote(cbuf.at[m], gbuf.at[m], cs.at[m], cr.at[m], section=below) for m in range(n_micro)]
    skips = [remote(kbuf.at[m], skbuf.at[m], ks.at[m], kr.at[m], section=mirror) for m in range(n_micro)]

    def forward(m):
        span = pl.ds(m * rows, rows)
        united = x[0, m].astype(F32) + jnp.dot(zbuf[m], w_skip[0], preferred_element_type=F32)
        recip = lax.rsqrt(jnp.mean(united * united, axis=-1, keepdims=True) + EPS)
        normed = (united * recip).astype(BF16)
        preact = contract(normed, w_in[0], ((1,), (1,)))
        sigma = jax.nn.sigmoid(preact)
        active = (preact * sigma).astype(BF16)
        ubuf[m] = united
        rbuf[m] = recip
        nbuf[span, :] = normed
        abuf[span, :] = active
        dbuf[m] = sigma * (1.0 + preact * (1.0 - sigma))
        return united, active

    @pl.when(sec < half)
    def _():
        levels = lax.broadcasted_iota(jnp.int32, (table.shape[0], rows), 0)
        for m in range(n_micro):
            onehot = (levels == ts[m : m + 1, :]).astype(F32).astype(BF16)
            zbuf[m] = contract(onehot, table[...], ((0,), (0,))).astype(BF16)
            united, active = forward(m)
            output = united + jnp.dot(active, w_out[0], preferred_element_type=F32)
            ybuf[m] = output.astype(BF16)
            if m == 0:
                pl.semaphore_wait(barrier, count)
            values[m].start()

    @pl.when(sec >= half - 1)
    def _():
        skbuf[...] = jnp.zeros_like(skbuf)

    @pl.when(sec >= half)
    def _():
        pl.semaphore_wait(barrier, count)

    for m in range(n_micro):

        @pl.when(sec >= half)
        def _():
            values[m].wait_recv()
            forward(m)

        @pl.when(sec == n_section - 1)
        def _():
            gbuf[m] = cot[m]

        @pl.when(sec < n_section - 1)
        def _():
            chains[m].wait_recv()

        @pl.when(sec < half - 1)
        def _():
            skips[m].wait_recv()

        span = pl.ds(m * rows, rows)
        grad_out = gbuf[m].astype(F32) + skbuf[m].astype(F32)
        grad_low = grad_out.astype(BF16)
        lowbuf[span, :] = grad_low
        grad_act = contract(grad_low, w_out[0], ((1,), (1,)))
        grad_pre = (grad_act * dbuf[m]).astype(BF16)
        gpbuf[span, :] = grad_pre
        grad_norm = jnp.dot(grad_pre, w_in[0], preferred_element_type=F32)
        united = ubuf[m]
        recip = rbuf[m]
        grad_united = (
            grad_out
            + recip * grad_norm
            - united * recip**3 * jnp.mean(grad_norm * united, axis=-1, keepdims=True)
        )
        low = grad_united.astype(BF16)
        ig[0, m] = low

        @pl.when(sec != half)
        def _():
            cbuf[m] = low

            @pl.when(sec > 0)
            def _():
                chains[m].start()

        @pl.when(sec >= half)
        def _():
            back = contract(low, w_skip[0], ((1,), (1,))).astype(BF16)

            @pl.when(sec == half)
            def _():
                cbuf[m] = (low.astype(F32) + back.astype(F32)).astype(BF16)
                chains[m].start()

            @pl.when(sec > half)
            def _():
                kbuf[m] = back
                skips[m].start()

    d_out = contract(abuf[...], lowbuf[...], ((0,), (0,)))
    d_in = contract(gpbuf[...], nbuf[...], ((0,), (0,)))
    d_skip = contract(
        zbuf[...].reshape(n_micro * rows, width), ig[0].reshape(n_micro * rows, width), ((0,), (0,))
    )

    if scatter:
        (acc, pbuf, precv, sbuf, rrecv, ps, pr, ss, sr) = rs
        fh = hidden // n_dp
        kh = width // n_dp
        acc[:, 0:fh, :] = d_in.reshape(n_dp, fh, width)
        acc[:, fh : 2 * fh, :] = d_out.reshape(n_dp, fh, width)
        acc[:, 2 * fh : 2 * fh + kh, :] = d_skip.reshape(n_dp, kh, width)
        first = []
        for t in range(pairs):
            pbuf[t] = acc[2 * t + 1 - core].astype(BF16)
            copy = remote(pbuf.at[t], precv.at[t], ps.at[t], pr.at[t], dp=mate)
            copy.start()
            first.append(copy)
        for copy in first:
            copy.wait_recv()
        second = []
        for k in range(1, pairs):
            t = lax.rem(place + k, pairs)
            sbuf[k] = (acc[2 * t + core] + precv[t].astype(F32)).astype(BF16)
            copy = remote(sbuf.at[k], rrecv.at[k], ss.at[k], sr.at[k], dp=2 * t + core)
            copy.start()
            second.append(copy)
        total = acc[dp] + precv[place].astype(F32)
        for k in range(1, pairs):
            second[k - 1].wait_recv()
            total = total + rrecv[k].astype(F32)
        g_in[...] = total[0:fh]
        g_out[...] = total[fh : 2 * fh]
        g_skip[...] = total[2 * fh : 2 * fh + kh]
        for copy in first + second:
            copy.wait_send()
    else:
        g_in[...] = d_in
        g_out[...] = d_out
        g_skip[...] = d_skip

    for m in range(n_micro):

        @pl.when(sec < half)
        def _():
            values[m].wait_send()

        @pl.when(sec > 0)
        def _():
            chains[m].wait_send()

        @pl.when(sec > half)
        def _():
            skips[m].wait_send()


def shards(n_section, n_dp, saved_inputs, timesteps, time_table, skip_weight, ff_in, ff_out, output_cotangent):
    n_micro, rows, width = output_cotangent.shape
    hidden = ff_in.shape[1]
    pairs = n_dp // 2
    scatter = n_dp % 2 == 0 and hidden % (16 * n_dp) == 0 and width % (8 * n_dp) == 0
    fh = hidden // n_dp if scatter else hidden
    kh = width // n_dp if scatter else width
    stack = 2 * fh + kh
    every = n_micro * rows
    low = pltpu.VMEM((n_micro, rows, width), BF16)
    scratch = [
        low,
        low,
        pltpu.VMEM((n_micro, rows, width), F32),
        pltpu.VMEM((n_micro, rows, 1), F32),
        pltpu.VMEM((every, width), BF16),
        pltpu.VMEM((every, hidden), BF16),
        pltpu.VMEM((n_micro, rows, hidden), F32),
        low,
        pltpu.VMEM((every, width), BF16),
        pltpu.VMEM((every, hidden), BF16),
        low,
        low,
        low,
    ] + [pltpu.SemaphoreType.DMA((n_micro,))] * 6
    if scatter:
        block = pltpu.VMEM((pairs, stack, width), BF16)
        scratch += [pltpu.VMEM((n_dp, stack, width), F32), block, block, block, block]
        scratch += [pltpu.SemaphoreType.DMA((pairs,))] * 4
    grad_store, grad_skip, grad_in, grad_out = pl.pallas_call(
        functools.partial(kernel, n_section, n_dp, scatter),
        out_shape=(
            jax.ShapeDtypeStruct(saved_inputs.shape, BF16),
            jax.ShapeDtypeStruct((kh, width), F32),
            jax.ShapeDtypeStruct((fh, width), F32),
            jax.ShapeDtypeStruct((fh, width), F32),
        ),
        in_specs=[pl.BlockSpec(memory_space=pltpu.VMEM)] * 7,
        out_specs=[pl.BlockSpec(memory_space=pltpu.VMEM)] * 4,
        scratch_shapes=scratch,
        compiler_params=pltpu.CompilerParams(
            collective_id=0, has_side_effects=True, vmem_limit_bytes=60 * 1024 * 1024
        ),
    )(saved_inputs, timesteps, time_table, skip_weight, ff_in, ff_out, output_cotangent)
    grad_skip = grad_skip.reshape(-1)
    if not scatter:
        grad_in, grad_out, grad_skip = (
            lax.psum_scatter(value, "dp", scatter_dimension=0, tiled=True)
            for value in (grad_in, grad_out, grad_skip)
        )
    return (grad_store, grad_skip[None], grad_in[None], grad_out[None])


def solution(mesh):
    in_specs = (
        P("section", None, "dp", None),
        P(None, "dp"),
        P(),
        P("section", None, None),
        P("section", None, None),
        P("section", None, None),
        P(None, "dp", None),
    )
    out_specs = (
        P("section", None, "dp", None),
        P("section", "dp"),
        P("section", "dp", None),
        P("section", "dp", None),
    )
    body = functools.partial(shards, mesh.shape["section"], mesh.shape["dp"])
    return jax.shard_map(body, mesh=mesh, in_specs=in_specs, out_specs=out_specs, check_vma=False)
```

time: 273 us -> 70.5 us (0.26)
  the two profiles are of different devices: /device:TPU:0 before, /device:TPU:9 now
where the time goes in v1:
time: 70.5 us; the launch traced here: 70.2 us
  Pallas kernels  57.9 us (82%)
  local copies, waits for them, and re-layouts  11.7 us (17%)
    pallas_call x1, Pallas kernels, shards(): pl.pallas_call(functools.partial(kernel, n_section, n_dp, scatter), out_s...  57.9 us
    unnamed x20, local copies, waits for them, and re-layouts  10.9 us

profile of v1, /device:TPU:9, one launch (start us, length us, event | category | flops | bytes accessed | tf_op | source)
XLA Modules:
  0.0 70.2 jit_solution(17995822815509018427)
XLA Ops:
  0.6 0.0 copy-start.2
  0.6 1.8 %copy.11.refs_0_ = bf16[1,2,128,320]{3,2,1,0:T(8,128)(2,1)} copy(bf16[1,2,128,320]{2,3,1,0:T(8,128)(2,1)} %param.7) | data formatting | bytes 327680 | tf_op args[0]
  2.4 0.0 copy-start
  2.4 1.8 %copy.15.refs_6_ = bf16[2,128,320]{2,1,0:T(8,128)(2,1)} copy(bf16[2,128,320]{1,2,0:T(8,128)(2,1)} %param.13) | data formatting | bytes 327680 | tf_op args[6]
  4.2 0.0 copy-done.2
  4.2 1.2 %copy.12.refs_2_ = bf16[1000,320]{1,0:T(8,128)(2,1)} copy(bf16[1000,320]{0,1:T(8,128)(2,1)S(1)} %copy-done.2) | data formatting | bytes 1280000 | tf_op args[2]
  5.4 0.0 copy-done
  5.4 0.0 copy-start.1
  5.4 1.3 %copy.13.refs_4_ = bf16[1,1280,320]{2,1,0:T(8,128)(2,1)} copy(bf16[1,1280,320]{1,2,0:T(8,128)(2,1)S(1)} %copy-done) | data formatting | bytes 1638400 | tf_op args[4]
  6.7 0.0 copy-done.1
  6.7 1.3 %copy.14.refs_5_ = bf16[1,1280,320]{2,1,0:T(8,128)(2,1)} copy(bf16[1,1280,320]{1,2,0:T(8,128)(2,1)S(1)} %copy-done.1) | data formatting | bytes 1638400 | tf_op args[5]
  8.1 57.9 %shard_map.102 = (bf16[1,2,128,320]{3,2,1,0:T(8,128)(2,1)}, f32[40,320]{1,0:T(8,128)}, f32[160,320]{1,0:T(8,128)}, f32[160,320]{1,0:T(8,128)}) custom-call(bf16[1,2,128,320]{3,2,1,0:T(8,128)(2,1)} %copy.11.refs_0_, s32[2,128]{1,0:T(2,128)} %refs_1_.1, bf16[1000,320]{1,0:T(8,128)(2,1)} %copy.12.refs_2_, bf16[1,320,320]{2,1,0:T(8,128)(2,1)} %refs_3_.1, ...), custom_call_target="tpu_custom_call" | custom-call | tf_op jit(solution)/shard_map/pallas_call | solution.py:245
  66.0 0.0 copy-start.4
  66.0 0.0 copy-start.5
  66.0 1.8 %copy.16 = bf16[1,2,128,320]{2,3,1,0:T(8,128)(2,1)} copy(bf16[1,2,128,320]{3,2,1,0:T(8,128)(2,1)} %get-tuple-element.12) | data formatting | bytes 327680
  67.8 0.0 copy-done.5
  67.8 0.7 %broadcast_in_dim_reshape.3 = f32[1,12800]{1,0:T(1,128)} reshape(f32[40,320]{1,0:T(8,128)S(1)} %copy-done.5) | data formatting | bytes 102400 | tf_op jit(solution)/shard_map/broadcast_in_dim;reshape | solution.py:266
  68.5 0.0 copy-done.4
  68.5 0.0 copy-start.3
  68.5 0.7 copy.19
  69.2 0.3 copy-done.3
  69.5 0.7 copy.20
Async XLA Ops:
  0.6 3.6 %copy-start.2 = (bf16[1000,320]{0,1:T(8,128)(2,1)S(1)}, bf16[1000,320]{0,1:T(8,128)(2,1)}, u32[]{:S(2)}) copy-start(bf16[1000,320]{0,1:T(8,128)(2,1)} %param.9) | copy-start | bytes 1920004
  2.4 3.0 %copy-start = (bf16[1,1280,320]{1,2,0:T(8,128)(2,1)S(1)}, bf16[1,1280,320]{1,2,0:T(8,128)(2,1)}, u32[]{:S(2)}) copy-start(bf16[1,1280,320]{1,2,0:T(8,128)(2,1)} %param.11) | copy-start | bytes 2457604
  5.4 1.3 %copy-start.1 = (bf16[1,1280,320]{1,2,0:T(8,128)(2,1)S(1)}, bf16[1,1280,320]{1,2,0:T(8,128)(2,1)}, u32[]{:S(2)}) copy-start(bf16[1,1280,320]{1,2,0:T(8,128)(2,1)} %param.12) | copy-start | bytes 2457604
  66.0 2.5 %copy-start.4 = (f32[160,320]{1,0:T(8,128)S(1)}, f32[160,320]{1,0:T(8,128)}, u32[]{:S(2)}) copy-start(f32[160,320]{1,0:T(8,128)} %get-tuple-element.10) | copy-start | bytes 614404
  66.0 1.8 %copy-start.5 = (f32[40,320]{1,0:T(8,128)S(1)}, f32[40,320]{1,0:T(8,128)}, u32[]{:S(2)}) copy-start(f32[40,320]{1,0:T(8,128)} %get-tuple-element.9) | copy-start | bytes 153604
  68.5 1.0 %copy-start.3 = (f32[160,320]{1,0:T(8,128)S(1)}, f32[160,320]{1,0:T(8,128)}, u32[]{:S(2)}) copy-start(f32[160,320]{1,0:T(8,128)} %get-tuple-element.11) | copy-start | bytes 614404

commit v2 on v1

v2 whole, which is shorter than its diff:
```python
import functools

import jax
import jax.numpy as jnp
from jax import lax
from jax.experimental import pallas as pl
from jax.experimental.pallas import tpu as pltpu
from jax.sharding import PartitionSpec as P

EPS = 1e-06
MESH = pl.DeviceIdType.MESH
F32 = jnp.float32
BF16 = jnp.bfloat16
LANES = 128
CHUNKS = 2


def contract(left, right, dims):
    return lax.dot_general(
        left, right, ((dims[0], dims[1]), ((), ())), preferred_element_type=jnp.float32
    )


def kernel(n_section, n_dp, scatter, *refs):
    (x, ts, table, w_skip, w_in, w_out, cot) = refs[:7]
    (ig, g_skip, g_in, g_out) = refs[7:11]
    (wsk_t, win_n, wout_n, zbuf, zall, ybuf, ubuf, rbuf, nbuf, abuf, dbuf) = refs[11:22]
    (gbuf, lowbuf, gpbuf, gall, cbuf, kbuf, skbuf) = refs[22:29]
    (vs, vr, cs, cr, ks, kr) = refs[29:35]
    rs = refs[35:]
    sec = lax.axis_index("section")
    dp = lax.axis_index("dp")
    n_micro, width, rows = cot.shape
    hidden = w_in.shape[2]
    half = n_section // 2
    pairs = n_dp // 2
    core = lax.rem(dp, 2)
    place = lax.div(dp, 2)
    mate = dp + 1 - 2 * core

    def remote(src, dst, send, recv, **where):
        return pltpu.make_async_remote_copy(
            src_ref=src, dst_ref=dst, send_sem=send, recv_sem=recv, device_id=where, device_id_type=MESH
        )

    barrier = pltpu.get_barrier_semaphore()
    count = 0
    for k in range(1, n_section):
        pl.semaphore_signal(
            barrier, inc=1, device_id={"section": lax.rem(sec + k, n_section)}, device_id_type=MESH
        )
        count += 1
    if scatter:
        pl.semaphore_signal(barrier, inc=1, device_id={"dp": mate}, device_id_type=MESH)
        count += 1
        for k in range(1, pairs):
            other = lax.rem(place + k, pairs) * 2 + core
            pl.semaphore_signal(barrier, inc=1, device_id={"dp": other}, device_id_type=MESH)
            count += 1

    mirror = n_section - 1 - sec
    below = lax.max(sec - 1, 0)
    values = [remote(ybuf.at[m], zbuf.at[m], vs.at[m], vr.at[m], section=mirror) for m in range(n_micro)]
    chains = [remote(cbuf.at[m], gbuf.at[m], cs.at[m], cr.at[m], section=below) for m in range(n_micro)]
    skips = [remote(kbuf.at[m], skbuf.at[m], ks.at[m], kr.at[m], section=mirror) for m in range(n_micro)]

    def forward(m):
        span = slice(m * rows, (m + 1) * rows)
        side = zbuf[m]
        zall[:, span] = side
        united = x[0, m].astype(F32) + jnp.dot(wsk_t[...], side, preferred_element_type=F32)
        recip = lax.rsqrt(jnp.mean(united * united, axis=0, keepdims=True) + EPS)
        normed = (united * recip).astype(BF16)
        preact = jnp.dot(win_n[...], normed, preferred_element_type=F32)
        sigma = jax.nn.sigmoid(preact)
        active = (preact * sigma).astype(BF16)
        ubuf[m] = united
        rbuf[m] = recip
        nbuf[:, span] = normed
        abuf[:, span] = active
        dbuf[m] = sigma * (1.0 + preact * (1.0 - sigma))
        return united, active

    wsk_t[...] = w_skip[0].T
    win_n[...] = w_in[0].T

    @pl.when(sec < half)
    def _():
        levels = lax.broadcasted_iota(jnp.int32, (table.shape[1], rows), 0)
        for m in range(n_micro):
            onehot = (levels == ts[m : m + 1, :]).astype(F32).astype(BF16)
            zbuf[m] = jnp.dot(table[...], onehot, preferred_element_type=F32).astype(BF16)
            united, active = forward(m)
            output = united + jnp.dot(w_out[0], active, preferred_element_type=F32)
            ybuf[m] = output.astype(BF16)
            if m == 0:
                pl.semaphore_wait(barrier, count)
            values[m].start()

    wout_n[...] = w_out[0].T

    @pl.when(sec >= half - 1)
    def _():
        skbuf[...] = jnp.zeros_like(skbuf)

    @pl.when(sec >= half)
    def _():
        pl.semaphore_wait(barrier, count)

    for m in range(n_micro):

        @pl.when(sec >= half)
        def _():
            values[m].wait_recv()
            forward(m)

        @pl.when(sec == n_section - 1)
        def _():
            gbuf[m] = cot[m]

        @pl.when(sec < n_section - 1)
        def _():
            chains[m].wait_recv()

        @pl.when(sec < half - 1)
        def _():
            skips[m].wait_recv()

        span = slice(m * rows, (m + 1) * rows)
        grad_out = gbuf[m].astype(F32) + skbuf[m].astype(F32)
        grad_low = grad_out.astype(BF16)
        lowbuf[:, span] = grad_low
        grad_act = jnp.dot(wout_n[...], grad_low, preferred_element_type=F32)
        grad_pre = (grad_act * dbuf[m]).astype(BF16)
        gpbuf[:, span] = grad_pre
        grad_norm = jnp.dot(w_in[0], grad_pre, preferred_element_type=F32)
        united = ubuf[m]
        recip = rbuf[m]
        grad_united = (
            grad_out
            + recip * grad_norm
            - united * recip**3 * jnp.mean(grad_norm * united, axis=0, keepdims=True)
        )
        low = grad_united.astype(BF16)

        @pl.when(sec != half)
        def _():
            cbuf[m] = low

            @pl.when(sec > 0)
            def _():
                chains[m].start()

        @pl.when(sec >= half)
        def _():
            back = jnp.dot(w_skip[0], low, preferred_element_type=F32).astype(BF16)

            @pl.when(sec == half)
            def _():
                cbuf[m] = (low.astype(F32) + back.astype(F32)).astype(BF16)
                chains[m].start()

            @pl.when(sec > half)
            def _():
                kbuf[m] = back
                skips[m].start()

        ig[0, m] = low
        gall[:, span] = low

    def product(left, right):
        return contract(left, right, ((1,), (1,)))

    if scatter:
        (acc, pbuf, precv, tot, sbuf_r, sbuf_l, in_r, in_l, ps, pr, rss, rsr, lss, lsr) = rs
        fh = hidden // n_dp
        kh = width // n_dp
        full = width // LANES
        tail = width % LANES
        stack = acc.shape[1]
        piece = stack // CHUNKS
        mix = 2 * full * fh
        order = []
        for t in range(pairs):
            k = pairs - 1 - t // 2 if t % 2 == 0 else t // 2
            order.append(k)
        first = [
            remote(pbuf.at[t], precv.at[t], ps.at[t], pr.at[t], dp=mate) for t in range(pairs)
        ]
        for t in order:
            fspan = slice(2 * t * fh, 2 * (t + 1) * fh)
            kspan = slice(2 * t * kh, 2 * (t + 1) * kh)
            d_out = product(abuf[fspan, :], lowbuf[...])
            d_in = product(gpbuf[fspan, :], nbuf[...])
            d_skip = product(zall[kspan, :], gall[...])
            for c in range(2):
                d = 2 * t + c
                for i in range(full):
                    cut = slice(i * LANES, (i + 1) * LANES)
                    acc[d, i * fh : (i + 1) * fh, :] = d_in[c * fh : (c + 1) * fh, cut]
                    acc[d, (full + i) * fh : (full + i + 1) * fh, :] = d_out[c * fh : (c + 1) * fh, cut]
                    at = mix + fh + i * kh
                    acc[d, at : at + kh, :] = d_skip[c * kh : (c + 1) * kh, cut]
                rest = slice(full * LANES, width)
                acc[d, mix : mix + fh, 0:tail] = d_in[c * fh : (c + 1) * fh, rest]
                acc[d, mix : mix + fh, tail : 2 * tail] = d_out[c * fh : (c + 1) * fh, rest]
                at = mix + fh + full * kh
                acc[d, at:stack, :] = jnp.zeros((stack - at, LANES), F32)
                acc[d, at : at + kh, 0:tail] = d_skip[c * kh : (c + 1) * kh, rest]
            pbuf[t] = acc[2 * t + 1 - core].astype(BF16)
            first[t].start()

        def hop(sbuf, into, send, recv, t, q, step):
            rows_of = pl.ds(q * piece, piece)
            at = jnp.clip(place + step, 0, pairs - 1) * 2 + core
            return remote(
                sbuf.at[t, rows_of], into.at[t, rows_of], send.at[t, q], recv.at[t, q], dp=at
            )

        def right(t, q):
            return hop(sbuf_r, in_r, rss, rsr, t, q, 1)

        def left(t, q):
            return hop(sbuf_l, in_l, lss, lsr, t, q, -1)

        for t in order:
            first[t].wait_recv()
            tot[t] = acc[2 * t + core] + precv[t].astype(F32)

        def push(copy, into, sbuf, t, inner):
            for q in range(CHUNKS):
                rows_of = pl.ds(q * piece, piece)

                @pl.when(inner)
                def _():
                    copy(t, q).wait_recv()
                    sbuf[t, rows_of] = (tot[t, rows_of] + into[t, rows_of].astype(F32)).astype(BF16)

                @pl.when(jnp.logical_not(inner))
                def _():
                    sbuf[t, rows_of] = tot[t, rows_of].astype(BF16)

                copy(t, q).start()

        def push_right(t):
            @pl.when(place < t)
            def _():
                push(right, in_r, sbuf_r, t, place > 0)

        def push_left(t):
            @pl.when(place > t)
            def _():
                push(left, in_l, sbuf_l, t, place < pairs - 1)

        for j in range(pairs - 1):

            @pl.when(2 * place < pairs)
            def _():
                push_right(pairs - 1 - j)
                push_left(j)

            @pl.when(2 * place >= pairs)
            def _():
                push_left(j)
                push_right(pairs - 1 - j)

        for q in range(CHUNKS):
            rows_of = pl.ds(q * piece, piece)

            @pl.when(place > 0)
            def _():
                right(place, q).wait_recv()
                tot[place, rows_of] += in_r[place, rows_of].astype(F32)

            @pl.when(place < pairs - 1)
            def _():
                left(place, q).wait_recv()
                tot[place, rows_of] += in_l[place, rows_of].astype(F32)

        for i in range(full):
            cut = slice(i * LANES, (i + 1) * LANES)
            g_in[:, cut] = tot[place, i * fh : (i + 1) * fh, :]
            g_out[:, cut] = tot[place, (full + i) * fh : (full + i + 1) * fh, :]
            at = mix + fh + i * kh
            g_skip[:, cut] = tot[place, at : at + kh, :]
        rest = slice(full * LANES, width)
        at = mix + fh + full * kh
        g_in[:, rest] = tot[place, mix : mix + fh, 0:tail]
        g_out[:, rest] = tot[place, mix : mix + fh, tail : 2 * tail]
        g_skip[:, rest] = tot[place, at : at + kh, 0:tail]
        for t in range(pairs):
            first[t].wait_send()

            @pl.when(place < t)
            def _():
                for q in range(CHUNKS):
                    right(t, q).wait_send()

            @pl.when(place > t)
            def _():
                for q in range(CHUNKS):
                    left(t, q).wait_send()
    else:
        g_in[...] = product(gpbuf[...], nbuf[...])
        g_out[...] = product(abuf[...], lowbuf[...])
        g_skip[...] = product(zall[...], gall[...])

    for m in range(n_micro):

        @pl.when(sec < half)
        def _():
            values[m].wait_send()

        @pl.when(sec > 0)
        def _():
            chains[m].wait_send()

        @pl.when(sec > half)
        def _():
            skips[m].wait_send()


def shards(n_section, n_dp, saved_inputs, timesteps, time_table, skip_weight, ff_in, ff_out, output_cotangent):
    n_micro, rows, width = output_cotangent.shape
    hidden = ff_in.shape[1]
    pairs = n_dp // 2
    aligned = hidden % (16 * n_dp) == 0 and width % (8 * n_dp) == 0
    scatter = n_dp % 2 == 0 and aligned and width % LANES == LANES // 2
    fh = hidden // n_dp if scatter else hidden
    kh = width // n_dp if scatter else width
    every = n_micro * rows
    low = pltpu.VMEM((n_micro, width, rows), BF16)
    wide = pltpu.VMEM((width, every), BF16)
    scratch = [
        pltpu.VMEM((width, width), BF16),
        pltpu.VMEM((hidden, width), BF16),
        pltpu.VMEM((hidden, width), BF16),
        low,
        wide,
        low,
        pltpu.VMEM((n_micro, width, rows), F32),
        pltpu.VMEM((n_micro, 1, rows), F32),
        wide,
        pltpu.VMEM((hidden, every), BF16),
        pltpu.VMEM((n_micro, hidden, rows), F32),
        low,
        wide,
        pltpu.VMEM((hidden, every), BF16),
        wide,
        low,
        low,
        low,
    ] + [pltpu.SemaphoreType.DMA((n_micro,))] * 6
    if scatter:
        full = width // LANES
        stack = (2 * full + 1) * fh + (full + 1) * kh
        stack = -(-stack // (16 * CHUNKS)) * 16 * CHUNKS
        block = pltpu.VMEM((pairs, stack, LANES), BF16)
        scratch += [pltpu.VMEM((n_dp, stack, LANES), F32), block, block]
        scratch += [pltpu.VMEM((pairs, stack, LANES), F32), block, block, block, block]
        scratch += [pltpu.SemaphoreType.DMA((pairs,))] * 2
        scratch += [pltpu.SemaphoreType.DMA((pairs, CHUNKS))] * 4
    turned = (
        jnp.swapaxes(saved_inputs, 2, 3),
        timesteps,
        time_table.T,
        skip_weight,
        jnp.swapaxes(ff_in, 1, 2),
        jnp.swapaxes(ff_out, 1, 2),
        jnp.swapaxes(output_cotangent, 1, 2),
    )
    grad_store, grad_skip, grad_in, grad_out = pl.pallas_call(
        functools.partial(kernel, n_section, n_dp, scatter),
        out_shape=(
            jax.ShapeDtypeStruct(turned[0].shape, BF16),
            jax.ShapeDtypeStruct((kh, width), F32),
            jax.ShapeDtypeStruct((fh, width), F32),
            jax.ShapeDtypeStruct((fh, width), F32),
        ),
        in_specs=[pl.BlockSpec(memory_space=pltpu.VMEM)] * 7,
        out_specs=[pl.BlockSpec(memory_space=pltpu.VMEM)] * 4,
        scratch_shapes=scratch,
        compiler_params=pltpu.CompilerParams(
            collective_id=0, has_side_effects=True, vmem_limit_bytes=60 * 1024 * 1024
        ),
    )(*turned)
    grad_store = jnp.swapaxes(grad_store, 2, 3)
    grad_skip = grad_skip.reshape(-1)
    if not scatter:
        grad_in, grad_out, grad_skip = (
            lax.psum_scatter(value, "dp", scatter_dimension=0, tiled=True)
            for value in (grad_in, grad_out, grad_skip)
        )
    return (grad_store, grad_skip[None], grad_in[None], grad_out[None])


def solution(mesh):
    in_specs = (
        P("section", None, "dp", None),
        P(None, "dp"),
        P(),
        P("section", None, None),
        P("section", None, None),
        P("section", None, None),
        P(None, "dp", None),
    )
    out_specs = (
        P("section", None, "dp", None),
        P("section", "dp"),
        P("section", "dp", None),
        P("section", "dp", None),
    )
    body = functools.partial(shards, mesh.shape["section"], mesh.shape["dp"])
    return jax.shard_map(body, mesh=mesh, in_specs=in_specs, out_specs=out_specs, check_vma=False)
```

time: 70.5 us -> 57.3 us (0.81)
  the two profiles are of different devices: /device:TPU:9 before, /device:TPU:0 now
where the time goes in v2:
time: 57.3 us; the launch traced here: 56.8 us
  Pallas kernels  51.2 us (89%)
  local copies, waits for them, and re-layouts  4.92 us (9%)
  between operations  0.65 us (1%)
    pallas_call x1, Pallas kernels, shards(): pl.pallas_call(functools.partial(kernel, n_section, n_dp, scatter), out_s...  51.2 us
    unnamed x7, local copies, waits for them, and re-layouts  3.32 us
    another operation x1, local copies, waits for them, and re-layouts, shards(): return (grad_store, grad_skip[None], grad_in[None], grad_out[None])  1.6 us

profile of v2, /device:TPU:0, one launch (start us, length us, event | category | flops | bytes accessed | tf_op | source)
XLA Modules:
  0.0 56.8 jit_solution(12539481951640071501)
XLA Ops:
  0.6 51.2 %shard_map.102 = (bf16[1,2,320,128]{3,2,1,0:T(8,128)(2,1)}, f32[40,320]{1,0:T(8,128)}, f32[160,320]{1,0:T(8,128)}, f32[160,320]{1,0:T(8,128)}) custom-call(bf16[1,2,320,128]{3,2,1,0:T(8,128)(2,1)} %bitcast.14, s32[2,128]{1,0:T(2,128)} %refs_1_.1, bf16[320,1000]{1,0:T(8,128)(2,1)} %bitcast.10, bf16[1,320,320]{2,1,0:T(8,128)(2,1)} %refs_3_.1, ...), custom_call_target="tpu_custom_call" | custom-call | tf_op jit(solution)/shard_map/pallas_call | solution.py:372
  51.8 0.0 copy-start.1
  51.9 1.6 %broadcast_in_dim_reshape.3 = f32[1,12800]{1,0:T(1,128)} reshape(f32[40,320]{1,0:T(8,128)} %get-tuple-element.9) | data formatting | bytes 102400 | tf_op jit(solution)/shard_map/broadcast_in_dim;reshape | solution.py:394
  53.5 1.6 %copy.14 = bf16[1,2,128,320]{2,3,1,0:T(8,128)(2,1)} copy(bf16[1,2,128,320]{2,3,1,0:T(8,128)(2,1)} %bitcast.13) | data formatting | bytes 327680
  55.0 0.0 copy-done.1
  55.0 0.0 copy-start
  55.0 0.7 %copy.15 = f32[1,160,320]{2,1,0:T(8,128)} copy(f32[1,160,320]{2,1,0:T(8,128)S(1)} %bitcast.12) | data formatting | bytes 409600
  55.7 0.3 copy-done
  56.1 0.7 %copy.16 = f32[1,160,320]{2,1,0:T(8,128)} copy(f32[1,160,320]{2,1,0:T(8,128)S(1)} %bitcast.11) | data formatting | bytes 409600
Async XLA Ops:
  51.8 3.2 %copy-start.1 = (f32[160,320]{1,0:T(8,128)S(1)}, f32[160,320]{1,0:T(8,128)}, u32[]{:S(2)}) copy-start(f32[160,320]{1,0:T(8,128)} %get-tuple-element.10) | copy-start | bytes 614404
  55.0 1.0 %copy-start = (f32[160,320]{1,0:T(8,128)S(1)}, f32[160,320]{1,0:T(8,128)}, u32[]{:S(2)}) copy-start(f32[160,320]{1,0:T(8,128)} %get-tuple-element.11) | copy-start | bytes 614404

commit v3 on v2

v3 whole, which is shorter than its diff:
```python
import functools

import jax
import jax.numpy as jnp
from jax import lax
from jax.experimental import pallas as pl
from jax.experimental.pallas import tpu as pltpu
from jax.sharding import PartitionSpec as P

EPS = 1e-06
MESH = pl.DeviceIdType.MESH
F32 = jnp.float32
BF16 = jnp.bfloat16
LANES = 128


def contract(left, right, dims):
    return lax.dot_general(
        left, right, ((dims[0], dims[1]), ((), ())), preferred_element_type=jnp.float32
    )


def kernel(n_section, n_dp, scatter, *refs):
    (x, ts, table, w_skip, w_in, w_out, cot) = refs[:7]
    (ig, g_out, g_in, g_skip) = refs[7:11]
    (wsk_t, win_n, wout_n, zbuf, zall, ybuf, ubuf, rbuf, nbuf, abuf, dbuf) = refs[11:22]
    (gbuf, lowbuf, gpbuf, gall, cbuf, kbuf, skbuf) = refs[22:29]
    (vs, vr, cs, cr, ks, kr) = refs[29:35]
    rs = refs[35:]
    sec = lax.axis_index("section")
    dp = lax.axis_index("dp")
    n_micro, width, rows = cot.shape
    hidden = w_in.shape[2]
    half = n_section // 2
    pairs = n_dp // 2
    core = lax.rem(dp, 2)
    place = lax.div(dp, 2)
    mate = dp + 1 - 2 * core

    def remote(src, dst, send, recv, **where):
        return pltpu.make_async_remote_copy(
            src_ref=src, dst_ref=dst, send_sem=send, recv_sem=recv, device_id=where, device_id_type=MESH
        )

    barrier = pltpu.get_barrier_semaphore()
    count = 0
    for k in range(1, n_section):
        pl.semaphore_signal(
            barrier, inc=1, device_id={"section": lax.rem(sec + k, n_section)}, device_id_type=MESH
        )
        count += 1
    if scatter:
        pl.semaphore_signal(barrier, inc=1, device_id={"dp": mate}, device_id_type=MESH)
        count += 1
        for k in range(1, pairs):
            other = lax.rem(place + k, pairs) * 2 + core
            pl.semaphore_signal(barrier, inc=1, device_id={"dp": other}, device_id_type=MESH)
            count += 1

    mirror = n_section - 1 - sec
    below = lax.max(sec - 1, 0)
    values = [remote(ybuf.at[m], zbuf.at[m], vs.at[m], vr.at[m], section=mirror) for m in range(n_micro)]
    chains = [remote(cbuf.at[m], gbuf.at[m], cs.at[m], cr.at[m], section=below) for m in range(n_micro)]
    skips = [remote(kbuf.at[m], skbuf.at[m], ks.at[m], kr.at[m], section=mirror) for m in range(n_micro)]

    def forward(m):
        span = slice(m * rows, (m + 1) * rows)
        side = zbuf[m]
        zall[:, span] = side
        united = x[0, m].astype(F32) + jnp.dot(wsk_t[...], side, preferred_element_type=F32)
        recip = lax.rsqrt(jnp.mean(united * united, axis=0, keepdims=True) + EPS)
        normed = (united * recip).astype(BF16)
        preact = jnp.dot(win_n[...], normed, preferred_element_type=F32)
        sigma = jax.nn.sigmoid(preact)
        active = (preact * sigma).astype(BF16)
        ubuf[m] = united
        rbuf[m] = recip
        nbuf[:, span] = normed
        abuf[:, span] = active
        dbuf[m] = sigma * (1.0 + preact * (1.0 - sigma))
        return united, active

    wsk_t[...] = w_skip[0].T
    win_n[...] = w_in[0].T

    @pl.when(sec < half)
    def _():
        levels = lax.broadcasted_iota(jnp.int32, (table.shape[1], rows), 0)
        for m in range(n_micro):
            onehot = (levels == ts[m : m + 1, :]).astype(F32).astype(BF16)
            zbuf[m] = jnp.dot(table[...], onehot, preferred_element_type=F32).astype(BF16)
            united, active = forward(m)
            output = united + jnp.dot(w_out[0], active, preferred_element_type=F32)
            ybuf[m] = output.astype(BF16)
            if m == 0:
                pl.semaphore_wait(barrier, count)
            values[m].start()

    wout_n[...] = w_out[0].T

    @pl.when(sec >= half - 1)
    def _():
        skbuf[...] = jnp.zeros_like(skbuf)

    @pl.when(sec >= half)
    def _():
        pl.semaphore_wait(barrier, count)

    def product(left, right):
        return contract(left, right, ((1,), (1,)))

    if scatter:
        parts = [rs[8 * p : 8 * p + 8] for p in range(3)]
        (ps, pr, rss, rsr, lss, lsr) = rs[24:]
        full = width // LANES
        tail = width % LANES
        factors = ((abuf, lowbuf, hidden // n_dp), (gpbuf, nbuf, hidden // n_dp), (zall, gall, width // n_dp))
        order = [pairs - 1 - t // 2 if t % 2 == 0 else t // 2 for t in range(pairs)]
        ends = (place == 0) | (place == pairs - 1)

        def first(p, t):
            return remote(parts[p][1].at[t], parts[p][2].at[t], ps.at[p, t], pr.at[p, t], dp=mate)

        def products(p):
            (acc, pbuf) = parts[p][:2]
            (left_ref, right_ref, n) = factors[p]
            used = full * n + n // 2
            for t in order:
                block = product(left_ref[2 * t * n : 2 * (t + 1) * n, :], right_ref[...])
                for k in range(2):
                    own = block[k * n : (k + 1) * n]
                    for i in range(full):
                        acc[2 * t + k, i * n : (i + 1) * n, :] = own[:, i * LANES : (i + 1) * LANES]
                    acc[2 * t + k, full * n : used, 0:tail] = own[0 : n // 2, full * LANES :]
                    acc[2 * t + k, full * n : used, tail:] = own[n // 2 :, full * LANES :]
                    if acc.shape[1] > used:
                        acc[2 * t + k, used:, :] = jnp.zeros((acc.shape[1] - used, LANES), F32)
                pbuf[t] = acc[2 * t + 1 - core].astype(BF16)
                first(p, t).start()

        def hop(sbuf, into, send, recv, p, t, step):
            at = jnp.clip(place + step, 0, pairs - 1) * 2 + core
            return remote(sbuf.at[t], into.at[t], send.at[p, t], recv.at[p, t], dp=at)

        def right(p, t):
            return hop(parts[p][4], parts[p][6], rss, rsr, p, t, 1)

        def left(p, t):
            return hop(parts[p][5], parts[p][7], lss, lsr, p, t, -1)

        def meet(p):
            for t in order:
                first(p, t).wait_recv()
                parts[p][3][t] = parts[p][0][2 * t + core] + parts[p][2][t].astype(F32)

        def push(copy, sbuf, into, total, p, t, inner):
            @pl.when(inner)
            def _():
                copy(p, t).wait_recv()
                sbuf[t] = (total[t] + into[t].astype(F32)).astype(BF16)

            @pl.when(jnp.logical_not(inner))
            def _():
                sbuf[t] = total[t].astype(BF16)

            copy(p, t).start()

        def push_right(group, t):
            @pl.when(place < t)
            def _():
                for p in group:
                    push(right, parts[p][4], parts[p][6], parts[p][3], p, t, place > 0)

        def push_left(group, t):
            @pl.when(place > t)
            def _():
                for p in group:
                    push(left, parts[p][5], parts[p][7], parts[p][3], p, t, place < pairs - 1)

        def line(group):
            for p in group:
                meet(p)
            for j in range(pairs - 1):

                @pl.when(2 * place < pairs)
                def _():
                    push_right(group, pairs - 1 - j)
                    push_left(group, j)

                @pl.when(2 * place >= pairs)
                def _():
                    push_left(group, j)
                    push_right(group, pairs - 1 - j)

    for m in range(n_micro):

        @pl.when(sec >= half)
        def _():
            values[m].wait_recv()
            forward(m)

        @pl.when(sec == n_section - 1)
        def _():
            gbuf[m] = cot[m]

        @pl.when(sec < n_section - 1)
        def _():
            chains[m].wait_recv()

        @pl.when(sec < half - 1)
        def _():
            skips[m].wait_recv()

        span = slice(m * rows, (m + 1) * rows)
        grad_out = gbuf[m].astype(F32) + skbuf[m].astype(F32)
        grad_low = grad_out.astype(BF16)
        lowbuf[:, span] = grad_low
        if scatter and m == n_micro - 1:

            @pl.when(sec == 0)
            def _():
                products(0)

                @pl.when(ends)
                def _():
                    line((0,))

        grad_act = jnp.dot(wout_n[...], grad_low, preferred_element_type=F32)
        grad_pre = (grad_act * dbuf[m]).astype(BF16)
        gpbuf[:, span] = grad_pre
        grad_norm = jnp.dot(w_in[0], grad_pre, preferred_element_type=F32)
        united = ubuf[m]
        recip = rbuf[m]
        grad_united = (
            grad_out
            + recip * grad_norm
            - united * recip**3 * jnp.mean(grad_norm * united, axis=0, keepdims=True)
        )
        low = grad_united.astype(BF16)

        @pl.when(sec != half)
        def _():
            cbuf[m] = low

            @pl.when(sec > 0)
            def _():
                chains[m].start()

        @pl.when(sec >= half)
        def _():
            back = jnp.dot(w_skip[0], low, preferred_element_type=F32).astype(BF16)

            @pl.when(sec == half)
            def _():
                cbuf[m] = (low.astype(F32) + back.astype(F32)).astype(BF16)
                chains[m].start()

            @pl.when(sec > half)
            def _():
                kbuf[m] = back
                skips[m].start()

        ig[0, m] = low
        gall[:, span] = low

    if scatter:

        @pl.when(sec > 0)
        def _():
            products(0)

        products(1)
        products(2)

        @pl.when((sec > 0) | jnp.logical_not(ends))
        def _():
            line((0,))

        line((1, 2))
        for p, result in enumerate((g_out, g_in, g_skip)):
            total = parts[p][3]

            @pl.when(place > 0)
            def _():
                right(p, place).wait_recv()
                total[place] += parts[p][6][place].astype(F32)

            @pl.when(place < pairs - 1)
            def _():
                left(p, place).wait_recv()
                total[place] += parts[p][7][place].astype(F32)

            result[...] = total[place]
            for t in range(pairs):
                first(p, t).wait_send()

                @pl.when(place < t)
                def _():
                    right(p, t).wait_send()

                @pl.when(place > t)
                def _():
                    left(p, t).wait_send()
    else:
        g_in[...] = product(gpbuf[...], nbuf[...])
        g_out[...] = product(abuf[...], lowbuf[...])
        g_skip[...] = product(zall[...], gall[...])

    for m in range(n_micro):

        @pl.when(sec < half)
        def _():
            values[m].wait_send()

        @pl.when(sec > 0)
        def _():
            chains[m].wait_send()

        @pl.when(sec > half)
        def _():
            skips[m].wait_send()


def finish(ig, p_out, p_in, p_skip, o_ig, o_skip, o_in, o_out, flat):
    o_ig[...] = ig[...]
    for packed, result in ((p_out, o_out), (p_in, o_in), (p_skip, flat)):
        (n, width) = result.shape
        full = width // LANES
        tail = width % LANES
        for i in range(full):
            result[:, i * LANES : (i + 1) * LANES] = packed[i * n : (i + 1) * n, :]
        used = full * n + n // 2
        result[0 : n // 2, full * LANES :] = packed[full * n : used, 0:tail]
        result[n // 2 :, full * LANES :] = packed[full * n : used, tail:]
    (n, width) = flat.shape
    for r in range(n):
        o_skip[:, r * width : (r + 1) * width] = flat[r : r + 1, :]


def shards(n_section, n_dp, saved_inputs, timesteps, time_table, skip_weight, ff_in, ff_out, output_cotangent):
    n_micro, rows, width = output_cotangent.shape
    hidden = ff_in.shape[1]
    pairs = n_dp // 2
    aligned = hidden % (16 * n_dp) == 0 and width % (8 * n_dp) == 0
    scatter = n_dp % 2 == 0 and aligned and width % LANES == LANES // 2
    fh = hidden // n_dp if scatter else hidden
    kh = width // n_dp if scatter else width
    every = n_micro * rows
    low = pltpu.VMEM((n_micro, width, rows), BF16)
    wide = pltpu.VMEM((width, every), BF16)
    scratch = [
        pltpu.VMEM((width, width), BF16),
        pltpu.VMEM((hidden, width), BF16),
        pltpu.VMEM((hidden, width), BF16),
        low,
        wide,
        low,
        pltpu.VMEM((n_micro, width, rows), F32),
        pltpu.VMEM((n_micro, 1, rows), F32),
        wide,
        pltpu.VMEM((hidden, every), BF16),
        pltpu.VMEM((n_micro, hidden, rows), F32),
        low,
        wide,
        pltpu.VMEM((hidden, every), BF16),
        wide,
        low,
        low,
        low,
    ] + [pltpu.SemaphoreType.DMA((n_micro,))] * 6
    sums = ((fh, width), (fh, width), (kh, width))
    if scatter:
        full = width // LANES
        sums = tuple((-(-(full * n + n // 2) // 16) * 16, LANES) for n in (fh, fh, kh))
        for n, lanes in sums:
            block = pltpu.VMEM((pairs, n, lanes), BF16)
            scratch += [pltpu.VMEM((n_dp, n, lanes), F32), block, block]
            scratch += [pltpu.VMEM((pairs, n, lanes), F32), block, block, block, block]
        scratch += [pltpu.SemaphoreType.DMA((3, pairs))] * 6
    turned = (
        jnp.swapaxes(saved_inputs, 2, 3),
        timesteps,
        time_table.T,
        skip_weight,
        jnp.swapaxes(ff_in, 1, 2),
        jnp.swapaxes(ff_out, 1, 2),
        jnp.swapaxes(output_cotangent, 1, 2),
    )
    vmem = pl.BlockSpec(memory_space=pltpu.VMEM)
    store_shape = jax.ShapeDtypeStruct(turned[0].shape, BF16)
    grad_store, grad_out, grad_in, grad_skip = pl.pallas_call(
        functools.partial(kernel, n_section, n_dp, scatter),
        out_shape=(store_shape,) + tuple(jax.ShapeDtypeStruct(shape, F32) for shape in sums),
        in_specs=[vmem] * 7,
        out_specs=[vmem] * 4,
        scratch_shapes=scratch,
        compiler_params=pltpu.CompilerParams(
            collective_id=0, has_side_effects=True, vmem_limit_bytes=44 * 1024 * 1024
        ),
    )(*turned)
    if scatter:
        grad_store, grad_skip, grad_in, grad_out = pl.pallas_call(
            finish,
            out_shape=(
                store_shape,
                jax.ShapeDtypeStruct((1, kh * width), F32),
                jax.ShapeDtypeStruct((fh, width), F32),
                jax.ShapeDtypeStruct((fh, width), F32),
            ),
            in_specs=[vmem] * 4,
            out_specs=[vmem] * 4,
            scratch_shapes=[pltpu.VMEM((kh, width), F32)],
            compiler_params=pltpu.CompilerParams(vmem_limit_bytes=8 * 1024 * 1024),
        )(grad_store, grad_out, grad_in, grad_skip)
    else:
        grad_in, grad_out, grad_skip = (
            lax.psum_scatter(value, "dp", scatter_dimension=0, tiled=True)
            for value in (grad_in, grad_out, grad_skip.reshape(-1))
        )
        grad_skip = grad_skip[None]
    grad_store = jnp.swapaxes(grad_store, 2, 3)
    return (grad_store, grad_skip, grad_in[None], grad_out[None])


def solution(mesh):
    in_specs = (
        P("section", None, "dp", None),
        P(None, "dp"),
        P(),
        P("section", None, None),
        P("section", None, None),
        P("section", None, None),
        P(None, "dp", None),
    )
    out_specs = (
        P("section", None, "dp", None),
        P("section", "dp"),
        P("section", "dp", None),
        P("section", "dp", None),
    )
    body = functools.partial(shards, mesh.shape["section"], mesh.shape["dp"])
    return jax.shard_map(body, mesh=mesh, in_specs=in_specs, out_specs=out_specs, check_vma=False)
```

time: 57.3 us -> 59.8 us (1.044)
  local copies, waits for them, and re-layouts: 4.92 us -> 6.82 us
  Pallas kernels: 51.2 us -> 52 us
    unnamed x7 -> x14, local copies, waits for them, and re-layouts: 3.32 us -> 6.82 us
    another operation x1 -> x0, local copies, waits for them, and re-layouts: 1.6 us -> none  [shards(): return (grad_store, grad_skip[None], grad_in[None], grad_out[None])]
    pallas_call x0 -> x1, Pallas kernels: none -> 0.94 us  [shards(): pl.pallas_call(finish, out_shape=(store_shape, jax.ShapeDtypeStruct((1, k...]
where the time goes in v3:
time: 59.8 us; the launch traced here: 59.5 us
  Pallas kernels  52 us (87%)
  local copies, waits for them, and re-layouts  6.82 us (11%)
  between operations  0.66 us (1%)
    pallas_call x1, Pallas kernels, shards(): pl.pallas_call(functools.partial(kernel, n_section, n_dp, scatter), out_s...  51.1 us
    unnamed x14, local copies, waits for them, and re-layouts  6.82 us

profile of v3, /device:TPU:0, one launch (start us, length us, event | category | flops | bytes accessed | tf_op | source)
XLA Modules:
  0.0 59.5 jit_solution(1712816897940610066)
XLA Ops:
  0.6 0.0 copy-start.6
  0.6 0.7 %copy-done.6 = s32[2,128]{1,0:T(2,128)S(1)} copy-done((s32[2,128]{1,0:T(2,128)S(1)}, s32[2,128]{1,0:T(2,128)}, u32[]{:S(2)}) %copy-start.6) | copy-done | bytes 1048
  1.3 0.0 copy-start
  1.3 1.1 %copy-done = bf16[1,1280,320]{1,2,0:T(8,128)(2,1)S(1)} copy-done((bf16[1,1280,320]{1,2,0:T(8,128)(2,1)S(1)}, bf16[1,1280,320]{1,2,0:T(8,128)(2,1)}, u32[]{:S(2)}) %copy-start) | copy-done | bytes 819224
  2.5 0.0 copy-start.1
  2.5 1.1 %copy-done.1 = bf16[1,1280,320]{1,2,0:T(8,128)(2,1)S(1)} copy-done((bf16[1,1280,320]{1,2,0:T(8,128)(2,1)S(1)}, bf16[1,1280,320]{1,2,0:T(8,128)(2,1)}, u32[]{:S(2)}) %copy-start.1) | copy-done | bytes 819224
  3.6 0.0 copy-start.2
  3.6 1.1 %copy-done.2 = bf16[1000,320]{0,1:T(8,128)(2,1)S(1)} copy-done((bf16[1000,320]{0,1:T(8,128)(2,1)S(1)}, bf16[1000,320]{0,1:T(8,128)(2,1)}, u32[]{:S(2)}) %copy-start.2) | copy-done | bytes 640024
  4.7 0.0 copy-start.3
  4.7 0.9 %copy-done.3 = bf16[1,320,320]{2,1,0:T(8,128)(2,1)S(1)} copy-done((bf16[1,320,320]{2,1,0:T(8,128)(2,1)S(1)}, bf16[1,320,320]{2,1,0:T(8,128)(2,1)}, u32[]{:S(2)}) %copy-start.3) | copy-done | bytes 204824
  5.6 0.0 copy-start.4
  5.6 0.9 %copy-done.4 = bf16[1,2,128,320]{2,3,1,0:T(8,128)(2,1)S(1)} copy-done((bf16[1,2,128,320]{2,3,1,0:T(8,128)(2,1)S(1)}, bf16[1,2,128,320]{2,3,1,0:T(8,128)(2,1)}, u32[]{:S(2)}) %copy-start.4) | copy-done | bytes 163864
  6.6 0.0 copy-start.5
  6.6 0.9 %copy-done.5 = bf16[2,128,320]{1,2,0:T(8,128)(2,1)S(1)} copy-done((bf16[2,128,320]{1,2,0:T(8,128)(2,1)S(1)}, bf16[2,128,320]{1,2,0:T(8,128)(2,1)}, u32[]{:S(2)}) %copy-start.5) | copy-done | bytes 163864
  7.5 51.1 %shard_map.102 = (bf16[1,2,320,128]{3,2,1,0:T(8,128)(2,1)S(1)}, f32[400,128]{1,0:T(8,128)S(1)}, f32[400,128]{1,0:T(8,128)S(1)}, f32[112,128]{1,0:T(8,128)S(1)}) custom-call(bf16[1,2,320,128]{3,2,1,0:T(8,128)(2,1)S(1)} %bitcast.11, s32[2,128]{1,0:T(2,128)S(1)} %copy-done.6, bf16[320,1000]{1,0:T(8,128)(2,1)S(1)} %bitcast.10, ...), custom_call_target="tpu_custom_call" | custom-call | tf_op jit(solution)/shard_map/pallas_call | solution.py:391
  58.5 0.9 %shard_map.103 = (bf16[1,2,320,128]{3,2,1,0:T(8,128)(2,1)}, f32[1,12800]{1,0:T(1,128)}, f32[160,320]{1,0:T(8,128)}, f32[160,320]{1,0:T(8,128)}) custom-call(bf16[1,2,320,128]{3,2,1,0:T(8,128)(2,1)S(1)} %get-tuple-element.12.ig, f32[400,128]{1,0:T(8,128)S(1)} %get-tuple-element.13.p_out, f32[400,128]{1,0:T(8,128)S(1)} %get-tuple-element.14.p_in, ...), custom_call_target="tpu_custom_call" | custom-call | tf_op jit(solution)/shard_map/pallas_call | solution.py:402
Async XLA Ops:
  0.6 0.7 %copy-start.6 = (s32[2,128]{1,0:T(2,128)S(1)}, s32[2,128]{1,0:T(2,128)}, u32[]{:S(2)}) copy-start(s32[2,128]{1,0:T(2,128)} %refs_1_.1) | copy-start | bytes 3076
  1.3 1.1 %copy-start = (bf16[1,1280,320]{1,2,0:T(8,128)(2,1)S(1)}, bf16[1,1280,320]{1,2,0:T(8,128)(2,1)}, u32[]{:S(2)}) copy-start(bf16[1,1280,320]{1,2,0:T(8,128)(2,1)} %param.11) | copy-start | bytes 2457604
  2.5 1.1 %copy-start.1 = (bf16[1,1280,320]{1,2,0:T(8,128)(2,1)S(1)}, bf16[1,1280,320]{1,2,0:T(8,128)(2,1)}, u32[]{:S(2)}) copy-start(bf16[1,1280,320]{1,2,0:T(8,128)(2,1)} %param.12) | copy-start | bytes 2457604
  3.6 1.1 %copy-start.2 = (bf16[1000,320]{0,1:T(8,128)(2,1)S(1)}, bf16[1000,320]{0,1:T(8,128)(2,1)}, u32[]{:S(2)}) copy-start(bf16[1000,320]{0,1:T(8,128)(2,1)} %param.9) | copy-start | bytes 1920004
  4.7 0.9 %copy-start.3 = (bf16[1,320,320]{2,1,0:T(8,128)(2,1)S(1)}, bf16[1,320,320]{2,1,0:T(8,128)(2,1)}, u32[]{:S(2)}) copy-start(bf16[1,320,320]{2,1,0:T(8,128)(2,1)} %refs_3_.1) | copy-start | bytes 614404
  5.6 0.9 %copy-start.4 = (bf16[1,2,128,320]{2,3,1,0:T(8,128)(2,1)S(1)}, bf16[1,2,128,320]{2,3,1,0:T(8,128)(2,1)}, u32[]{:S(2)}) copy-start(bf16[1,2,128,320]{2,3,1,0:T(8,128)(2,1)} %param.7) | copy-start | bytes 491524
  6.6 0.9 %copy-start.5 = (bf16[2,128,320]{1,2,0:T(8,128)(2,1)S(1)}, bf16[2,128,320]{1,2,0:T(8,128)(2,1)}, u32[]{:S(2)}) copy-start(bf16[2,128,320]{1,2,0:T(8,128)(2,1)} %param.13) | copy-start | bytes 491524

commit v4 on v2

--- a/solution.py
+++ b/solution.py
@@ -22,12 +22,21 @@
 
 
 def kernel(n_section, n_dp, scatter, *refs):
-    (x, ts, table, w_skip, w_in, w_out, cot) = refs[:7]
-    (ig, g_skip, g_in, g_out) = refs[7:11]
+    outside = refs[:7]
+    results = 2 if scatter else 4
+    ig = refs[7]
+    sums = refs[8 : 7 + results]
+    refs = refs[:11] + refs[7 + results :]
     (wsk_t, win_n, wout_n, zbuf, zall, ybuf, ubuf, rbuf, nbuf, abuf, dbuf) = refs[11:22]
     (gbuf, lowbuf, gpbuf, gall, cbuf, kbuf, skbuf) = refs[22:29]
     (vs, vr, cs, cr, ks, kr) = refs[29:35]
-    rs = refs[35:]
+    inside = refs[35:42]
+    (x, ts, table, w_skip, w_in, w_out, cot) = inside
+    loaded = refs[42]
+    rs = refs[43:]
+    loads = [pltpu.make_async_copy(outside[i], inside[i], loaded.at[i]) for i in range(7)]
+    for i in (3, 4, 1, 2, 0, 5, 6):
+        loads[i].start()
     sec = lax.axis_index("section")
     dp = lax.axis_index("dp")
     n_micro, width, rows = cot.shape
@@ -81,8 +90,12 @@
         dbuf[m] = sigma * (1.0 + preact * (1.0 - sigma))
         return united, active
 
+    loads[3].wait()
     wsk_t[...] = w_skip[0].T
+    loads[4].wait()
     win_n[...] = w_in[0].T
+    for i in (1, 2, 0, 5):
+        loads[i].wait()
 
     @pl.when(sec < half)
     def _():
@@ -98,6 +111,7 @@
             values[m].start()
 
     wout_n[...] = w_out[0].T
+    loads[6].wait()
 
     @pl.when(sec >= half - 1)
     def _():
@@ -277,17 +291,7 @@
                 left(place, q).wait_recv()
                 tot[place, rows_of] += in_l[place, rows_of].astype(F32)
 
-        for i in range(full):
-            cut = slice(i * LANES, (i + 1) * LANES)
-            g_in[:, cut] = tot[place, i * fh : (i + 1) * fh, :]
-            g_out[:, cut] = tot[place, (full + i) * fh : (full + i + 1) * fh, :]
-            at = mix + fh + i * kh
-            g_skip[:, cut] = tot[place, at : at + kh, :]
-        rest = slice(full * LANES, width)
-        at = mix + fh + full * kh
-        g_in[:, rest] = tot[place, mix : mix + fh, 0:tail]
-        g_out[:, rest] = tot[place, mix : mix + fh, tail : 2 * tail]
-        g_skip[:, rest] = tot[place, at : at + kh, 0:tail]
+        sums[0][...] = tot[place]
         for t in range(pairs):
             first[t].wait_send()
 
@@ -301,9 +305,9 @@
                 for q in range(CHUNKS):
                     left(t, q).wait_send()
     else:
-        g_in[...] = product(gpbuf[...], nbuf[...])
-        g_out[...] = product(abuf[...], lowbuf[...])
-        g_skip[...] = product(zall[...], gall[...])
+        sums[0][...] = product(gpbuf[...], nbuf[...])
+        sums[1][...] = product(abuf[...], lowbuf[...])
+        sums[2][...] = product(zall[...], gall[...])
 
     for m in range(n_micro):
 
@@ -318,6 +322,28 @@
         @pl.when(sec > half)
         def _():
             skips[m].wait_send()
+
+
+def finish(ig, packed, o_ig, o_skip, o_in, o_out, flat):
+    o_ig[...] = ig[...]
+    (fh, width) = o_in.shape
+    kh = flat.shape[0]
+    full = width // LANES
+    tail = width % LANES
+    mix = 2 * full * fh
+    for i in range(full):
+        cut = slice(i * LANES, (i + 1) * LANES)
+        o_in[:, cut] = packed[i * fh : (i + 1) * fh, :]
+        o_out[:, cut] = packed[(full + i) * fh : (full + i + 1) * fh, :]
+        at = mix + fh + i * kh
+        flat[:, cut] = packed[at : at + kh, :]
+    rest = slice(full * LANES, width)
+    at = mix + fh + full * kh
+    o_in[:, rest] = packed[mix : mix + fh, 0:tail]
+    o_out[:, rest] = packed[mix : mix + fh, tail : 2 * tail]
+    flat[:, rest] = packed[at : at + kh, 0:tail]
+    for r in range(kh):
+        o_skip[:, r * width : (r + 1) * width] = flat[r : r + 1, :]
 
 
 def shards(n_section, n_dp, saved_inputs, timesteps, time_table, skip_weight, ff_in, ff_out, output_cotangent):
@@ -351,6 +377,18 @@
         low,
         low,
     ] + [pltpu.SemaphoreType.DMA((n_micro,))] * 6
+    turned = (
+        jnp.swapaxes(saved_inputs, 2, 3),
+        timesteps,
+        time_table.T,
+        skip_weight,
+        jnp.swapaxes(ff_in, 1, 2),
+        jnp.swapaxes(ff_out, 1, 2),
+        jnp.swapaxes(output_cotangent, 1, 2),
+    )
+    scratch += [pltpu.VMEM(value.shape, value.dtype) for value in turned]
+    scratch += [pltpu.SemaphoreType.DMA((7,))]
+    sums = ((fh, width), (fh, width), (kh, width))
     if scatter:
         full = width // LANES
         stack = (2 * full + 1) * fh + (full + 1) * kh
@@ -360,38 +398,41 @@
         scratch += [pltpu.VMEM((pairs, stack, LANES), F32), block, block, block, block]
         scratch += [pltpu.SemaphoreType.DMA((pairs,))] * 2
         scratch += [pltpu.SemaphoreType.DMA((pairs, CHUNKS))] * 4
-    turned = (
-        jnp.swapaxes(saved_inputs, 2, 3),
-        timesteps,
-        time_table.T,
-        skip_weight,
-        jnp.swapaxes(ff_in, 1, 2),
-        jnp.swapaxes(ff_out, 1, 2),
-        jnp.swapaxes(output_cotangent, 1, 2),
-    )
-    grad_store, grad_skip, grad_in, grad_out = pl.pallas_call(
+        sums = ((stack, LANES),)
+    vmem = pl.BlockSpec(memory_space=pltpu.VMEM)
+    store_shape = jax.ShapeDtypeStruct(turned[0].shape, BF16)
+    grad_store, *grads = pl.pallas_call(
         functools.partial(kernel, n_section, n_dp, scatter),
-        out_shape=(
-            jax.ShapeDtypeStruct(turned[0].shape, BF16),
-            jax.ShapeDtypeStruct((kh, width), F32),
-            jax.ShapeDtypeStruct((fh, width), F32),
-            jax.ShapeDtypeStruct((fh, width), F32),
-        ),
-        in_specs=[pl.BlockSpec(memory_space=pltpu.VMEM)] * 7,
-        out_specs=[pl.BlockSpec(memory_space=pltpu.VMEM)] * 4,
+        out_shape=(store_shape,) + tuple(jax.ShapeDtypeStruct(shape, F32) for shape in sums),
+        in_specs=[pl.BlockSpec(memory_space=pltpu.HBM)] * 7,
+        out_specs=[vmem] * (1 + len(sums)),
         scratch_shapes=scratch,
         compiler_params=pltpu.CompilerParams(
-            collective_id=0, has_side_effects=True, vmem_limit_bytes=60 * 1024 * 1024
+            collective_id=0, has_side_effects=True, vmem_limit_bytes=60000 * 1024
         ),
     )(*turned)
-    grad_store = jnp.swapaxes(grad_store, 2, 3)
-    grad_skip = grad_skip.reshape(-1)
-    if not scatter:
+    if scatter:
+        grad_store, grad_skip, grad_in, grad_out = pl.pallas_call(
+            finish,
+            out_shape=(
+                store_shape,
+                jax.ShapeDtypeStruct((1, kh * width), F32),
+                jax.ShapeDtypeStruct((fh, width), F32),
+                jax.ShapeDtypeStruct((fh, width), F32),
+            ),
+            in_specs=[vmem] * 2,
+            out_specs=[vmem] * 4,
+            scratch_shapes=[pltpu.VMEM((kh, width), F32)],
+            compiler_params=pltpu.CompilerParams(vmem_limit_bytes=60 * 1024 * 1024),
+        )(grad_store, *grads)
+    else:
         grad_in, grad_out, grad_skip = (
             lax.psum_scatter(value, "dp", scatter_dimension=0, tiled=True)
-            for value in (grad_in, grad_out, grad_skip)
+            for value in (grads[0], grads[1], grads[2].reshape(-1))
         )
-    return (grad_store, grad_skip[None], grad_in[None], grad_out[None])
+        grad_skip = grad_skip[None]
+    grad_store = jnp.swapaxes(grad_store, 2, 3)
+    return (grad_store, grad_skip, grad_in[None], grad_out[None])
 
 
 def solution(mesh):

time: 57.3 us -> 53.1 us (0.927)
  local copies, waits for them, and re-layouts: 4.92 us -> 0 us
  Pallas kernels: 51.2 us -> 52 us
    unnamed x7 -> x0, local copies, waits for them, and re-layouts: 3.32 us -> none
    pallas_call x0 -> x1, Pallas kernels: none -> 2.01 us  [shards(): pl.pallas_call(finish, out_shape=(store_shape, jax.ShapeDtypeStruct((1, k...]
    another operation x1 -> x0, local copies, waits for them, and re-layouts: 1.6 us -> none  [shards(): return (grad_store, grad_skip[None], grad_in[None], grad_out[None])]
    pallas_call x1, Pallas kernels: 51.2 us -> 50 us  [shards(): pl.pallas_call(functools.partial(kernel, n_section, n_dp, scatter), out_s...]
where the time goes in v4:
time: 53.1 us; the launch traced here: 52.7 us
  Pallas kernels  52 us (98%)
  between operations  0.64 us (1%)
    pallas_call x1, Pallas kernels, shards(): pl.pallas_call(functools.partial(kernel, n_section, n_dp, scatter), out_s...  50 us
    pallas_call x1, Pallas kernels, shards(): pl.pallas_call(finish, out_shape=(store_shape, jax.ShapeDtypeStruct((1, k...  2.01 us

profile of v4, /device:TPU:0, one launch (start us, length us, event | category | flops | bytes accessed | tf_op | source)
XLA Modules:
  0.0 52.7 jit_solution(5347844065214580358)
XLA Ops:
  0.6 50.0 %shard_map.102 = (bf16[1,2,320,128]{3,2,1,0:T(8,128)(2,1)}, f32[928,128]{1,0:T(8,128)}) custom-call(bf16[1,2,320,128]{3,2,1,0:T(8,128)(2,1)} %bitcast.11, s32[2,128]{1,0:T(2,128)} %refs_1_.1, bf16[320,1000]{1,0:T(8,128)(2,1)} %bitcast.10, bf16[1,320,320]{2,1,0:T(8,128)(2,1)} %refs_3_.1, bf16[1,320,1280]{2,1,0:T(8,128)(2,1)} %bitcast.8, ...), custom_call_target="tpu_custom_call" | custom-call | tf_op jit(solution)/shard_map/pallas_call | solution.py:404
  50.7 2.0 %shard_map.103 = (bf16[1,2,320,128]{3,2,1,0:T(8,128)(2,1)}, f32[1,12800]{1,0:T(1,128)}, f32[160,320]{1,0:T(8,128)}, f32[160,320]{1,0:T(8,128)}) custom-call(bf16[1,2,320,128]{3,2,1,0:T(8,128)(2,1)} %get-tuple-element.10.ig, f32[928,128]{1,0:T(8,128)} %get-tuple-element.11.packed), custom_call_target="tpu_custom_call" | custom-call | tf_op jit(solution)/shard_map/pallas_call | solution.py:415

commit v5 on v4

--- a/solution.py
+++ b/solution.py
@@ -201,7 +201,30 @@
         first = [
             remote(pbuf.at[t], precv.at[t], ps.at[t], pr.at[t], dp=mate) for t in range(pairs)
         ]
-        for t in order:
+        def hop(sbuf, into, send, recv, t, q, step):
+            rows_of = pl.ds(q * piece, piece)
+            at = jnp.clip(place + step, 0, pairs - 1) * 2 + core
+            return remote(
+                sbuf.at[t, rows_of], into.at[t, rows_of], send.at[t, q], recv.at[t, q], dp=at
+            )
+
+        def right(t, q):
+            return hop(sbuf_r, in_r, rss, rsr, t, q, 1)
+
+        def left(t, q):
+            return hop(sbuf_l, in_l, lss, lsr, t, q, -1)
+
+        def meet(t):
+            first[t].wait_recv()
+            tot[t] = acc[2 * t + core] + precv[t].astype(F32)
+
+        def open_line(copy, sbuf, t):
+            for q in range(CHUNKS):
+                rows_of = pl.ds(q * piece, piece)
+                sbuf[t, rows_of] = tot[t, rows_of].astype(BF16)
+                copy(t, q).start()
+
+        for i_t, t in enumerate(order):
             fspan = slice(2 * t * fh, 2 * (t + 1) * fh)
             kspan = slice(2 * t * kh, 2 * (t + 1) * kh)
             d_out = product(abuf[fspan, :], lowbuf[...])
@@ -223,23 +246,20 @@
                 acc[d, at : at + kh, 0:tail] = d_skip[c * kh : (c + 1) * kh, rest]
             pbuf[t] = acc[2 * t + 1 - core].astype(BF16)
             first[t].start()
-
-        def hop(sbuf, into, send, recv, t, q, step):
-            rows_of = pl.ds(q * piece, piece)
-            at = jnp.clip(place + step, 0, pairs - 1) * 2 + core
-            return remote(
-                sbuf.at[t, rows_of], into.at[t, rows_of], send.at[t, q], recv.at[t, q], dp=at
-            )
-
-        def right(t, q):
-            return hop(sbuf_r, in_r, rss, rsr, t, q, 1)
-
-        def left(t, q):
-            return hop(sbuf_l, in_l, lss, lsr, t, q, -1)
-
-        for t in order:
-            first[t].wait_recv()
-            tot[t] = acc[2 * t + core] + precv[t].astype(F32)
+            if i_t == 1:
+                meet(order[0])
+                meet(order[1])
+
+                @pl.when(place == 0)
+                def _():
+                    open_line(right, sbuf_r, pairs - 1)
+
+                @pl.when(place == pairs - 1)
+                def _():
+                    open_line(left, sbuf_l, 0)
+
+        for t in order[2:]:
+            meet(t)
 
         def push(copy, into, sbuf, t, inner):
             for q in range(CHUNKS):
@@ -257,12 +277,12 @@
                 copy(t, q).start()
 
         def push_right(t):
-            @pl.when(place < t)
+            @pl.when((place < t) & (place > 0) if t == pairs - 1 else place < t)
             def _():
                 push(right, in_r, sbuf_r, t, place > 0)
 
         def push_left(t):
-            @pl.when(place > t)
+            @pl.when((place > t) & (place < pairs - 1) if t == 0 else place > t)
             def _():
                 push(left, in_l, sbuf_l, t, place < pairs - 1)
 
@@ -351,7 +371,7 @@
     hidden = ff_in.shape[1]
     pairs = n_dp // 2
     aligned = hidden % (16 * n_dp) == 0 and width % (8 * n_dp) == 0
-    scatter = n_dp % 2 == 0 and aligned and width % LANES == LANES // 2
+    scatter = n_dp % 2 == 0 and pairs > 1 and aligned and width % LANES == LANES // 2
     fh = hidden // n_dp if scatter else hidden
     kh = width // n_dp if scatter else width
     every = n_micro * rows

time: 53.1 us -> 51.8 us (0.976)
  Pallas kernels: 52 us -> 50.6 us
    pallas_call x1, Pallas kernels: 50 us -> 48.6 us  [shards(): pl.pallas_call(functools.partial(kernel, n_section, n_dp, scatter), out_s...]
where the time goes in v5:
time: 51.8 us; the launch traced here: 51.2 us
  Pallas kernels  50.6 us (98%)
  between operations  0.64 us (1%)
    pallas_call x1, Pallas kernels, shards(): pl.pallas_call(functools.partial(kernel, n_section, n_dp, scatter), out_s...  48.6 us
    pallas_call x1, Pallas kernels, shards(): pl.pallas_call(finish, out_shape=(store_shape, jax.ShapeDtypeStruct((1, k...  2.01 us

profile of v5, /device:TPU:0, one launch (start us, length us, event | category | flops | bytes accessed | tf_op | source)
XLA Modules:
  0.0 51.2 jit_solution(12671676498636532140)
XLA Ops:
  0.6 48.6 %shard_map.102 = (bf16[1,2,320,128]{3,2,1,0:T(8,128)(2,1)}, f32[928,128]{1,0:T(8,128)}) custom-call(bf16[1,2,320,128]{3,2,1,0:T(8,128)(2,1)} %bitcast.11, s32[2,128]{1,0:T(2,128)} %refs_1_.1, bf16[320,1000]{1,0:T(8,128)(2,1)} %bitcast.10, bf16[1,320,320]{2,1,0:T(8,128)(2,1)} %refs_3_.1, bf16[1,320,1280]{2,1,0:T(8,128)(2,1)} %bitcast.8, ...), custom_call_target="tpu_custom_call" | custom-call | tf_op jit(solution)/shard_map/pallas_call | solution.py:424
  49.2 2.0 %shard_map.103 = (bf16[1,2,320,128]{3,2,1,0:T(8,128)(2,1)}, f32[1,12800]{1,0:T(1,128)}, f32[160,320]{1,0:T(8,128)}, f32[160,320]{1,0:T(8,128)}) custom-call(bf16[1,2,320,128]{3,2,1,0:T(8,128)(2,1)} %get-tuple-element.10.ig, f32[928,128]{1,0:T(8,128)} %get-tuple-element.11.packed), custom_call_target="tpu_custom_call" | custom-call | tf_op jit(solution)/shard_map/pallas_call | solution.py:435

commit v6 on v5

--- a/solution.py
+++ b/solution.py
@@ -12,7 +12,7 @@
 F32 = jnp.float32
 BF16 = jnp.bfloat16
 LANES = 128
-CHUNKS = 2
+CHUNKS = 1
 
 
 def contract(left, right, dims):

time: 51.8 us -> 56.4 us (1.089)
  Pallas kernels: 50.6 us -> 55.6 us
    pallas_call x1, Pallas kernels: 48.6 us -> 53.6 us  [shards(): pl.pallas_call(functools.partial(kernel, n_section, n_dp, scatter), out_s...]
where the time goes in v6:
time: 56.4 us; the launch traced here: 56.2 us
  Pallas kernels  55.6 us (99%)
  between operations  0.64 us (1%)
    pallas_call x1, Pallas kernels, shards(): pl.pallas_call(functools.partial(kernel, n_section, n_dp, scatter), out_s...  53.6 us
    pallas_call x1, Pallas kernels, shards(): pl.pallas_call(finish, out_shape=(store_shape, jax.ShapeDtypeStruct((1, k...  2.01 us

profile of v6, /device:TPU:0, one launch (start us, length us, event | category | flops | bytes accessed | tf_op | source)
XLA Modules:
  0.0 56.2 jit_solution(12881543183489543353)
XLA Ops:
  0.6 53.6 %shard_map.102 = (bf16[1,2,320,128]{3,2,1,0:T(8,128)(2,1)}, f32[928,128]{1,0:T(8,128)}) custom-call(bf16[1,2,320,128]{3,2,1,0:T(8,128)(2,1)} %bitcast.11, s32[2,128]{1,0:T(2,128)} %refs_1_.1, bf16[320,1000]{1,0:T(8,128)(2,1)} %bitcast.10, bf16[1,320,320]{2,1,0:T(8,128)(2,1)} %refs_3_.1, bf16[1,320,1280]{2,1,0:T(8,128)(2,1)} %bitcast.8, ...), custom_call_target="tpu_custom_call" | custom-call | tf_op jit(solution)/shard_map/pallas_call | solution.py:424
  54.2 2.0 %shard_map.103 = (bf16[1,2,320,128]{3,2,1,0:T(8,128)(2,1)}, f32[1,12800]{1,0:T(1,128)}, f32[160,320]{1,0:T(8,128)}, f32[160,320]{1,0:T(8,128)}) custom-call(bf16[1,2,320,128]{3,2,1,0:T(8,128)(2,1)} %get-tuple-element.10.ig, f32[928,128]{1,0:T(8,128)} %get-tuple-element.11.packed), custom_call_target="tpu_custom_call" | custom-call | tf_op jit(solution)/shard_map/pallas_call | solution.py:435
